TPU v7x, 1024 devices: a whole 8x8x8 slice. The times are simulated.
1024 devices in a mesh: dp: 8 (over y), expert: 8 (over z), tensor: 16 (over x, core).
Axes of the slice: x: 8, y: 8, z: 8, core: 2. Of those that a mesh axis runs over, the one named last changes fastest.
Arguments:
- grad_out: bfloat16 [8192, 6144], P(('dp', 'expert'), 'tensor'), may hold values from -0.1875 to 0.1875
- expert_ids: int32 [8192, 2], P(('dp', 'expert')), may hold values from 0 to 7, all different within a row; in each aligned block of 128 rows (0 to 127, 128 to 255, ...) at most 64 rows name the same one
- route_gates: float32 [8192, 2], P(('dp', 'expert')), may hold values from 0.1 to 1
- saved_hidden: bfloat16 [8, 2048, 16384], P('expert', 'dp', 'tensor'), may hold values from -6 to 6
Outputs:
- weight_grad: bfloat16 [8, 16384, 6144], P('expert', 'tensor', 'dp')
Inputs may be any that keep to these rules, and one draw needn't show every extreme that they name: `expert_ids`: each row names 2 different experts. Among the rows of one device no expert is named by more than 64 rows, and every expert is named somewhere.
All inputs are finite; a program needn't handle non-finite values.
Results may differ from a plain program's by a relative error of at most 0.0049.
Values may be sent and summed in bfloat16 or wider, within the bound.
No kernel may reach another device: no remote copies, remote signals or barrier semaphores. Data moves between devices by JAX's collectives and lax.ppermute only.
A program may use at most 32 MiB of HBM per device.

v0:
```python
import jax
import jax.numpy as jnp
from jax import lax
from jax.experimental import pallas as pl
from jax.experimental.pallas import tpu as pltpu
from jax.sharding import PartitionSpec as P


CAP = 32
CORES = 2


def select_body(experts, ids_ref, gates_ref, grads_ref, out_ref):
    tokens = ids_ref.shape[1]
    ids, gates = ids_ref[...], gates_ref[...]
    expert = lax.broadcasted_iota(jnp.int32, (experts, tokens), 0)
    named = jnp.zeros((experts, tokens), jnp.float32)
    gate = jnp.zeros((experts, tokens), jnp.float32)
    for k in range(ids_ref.shape[0]):
        hit = ids[k : k + 1, :] == expert
        named = jnp.where(hit, 1.0, named)
        gate = jnp.where(hit, gates[k : k + 1, :], gate)
    earlier = lax.broadcasted_iota(jnp.int32, (tokens, tokens), 0) < lax.broadcasted_iota(
        jnp.int32, (tokens, tokens), 1
    )
    rank = lax.dot_general(
        named.astype(jnp.bfloat16),
        earlier.astype(jnp.bfloat16),
        (((1,), (0,)), ((), ())),
        preferred_element_type=jnp.float32,
    )
    rank = jnp.where(named > 0, rank, -1.0).astype(jnp.int32)
    slot = lax.broadcasted_iota(jnp.int32, (CAP, tokens), 0)
    grads = grads_ref[...]
    for e in range(experts):
        hit = rank[e : e + 1, :] == slot
        weight = jnp.sum(jnp.where(hit, gate[e : e + 1, :], 0.0), axis=1, keepdims=True)
        chosen = jnp.where(hit, 1.0, 0.0).astype(jnp.bfloat16)
        picked = lax.dot_general(
            chosen, grads, (((1,), (0,)), ((), ())), preferred_element_type=jnp.float32
        )
        out_ref[e] = (picked * weight).astype(out_ref.dtype)


def part_body(at, in_ref, out_ref):
    out_ref[...] = in_ref[at : at + out_ref.shape[0], :]


def part(array, at, size):
    vmem = pl.BlockSpec(memory_space=pltpu.VMEM)
    return pl.pallas_call(
        lambda *refs: part_body(at, *refs),
        out_shape=pltpu.VMEM((size, array.shape[1]), array.dtype),
        in_specs=[vmem],
        out_specs=vmem,
        compiler_params=pltpu.CompilerParams(vmem_limit_bytes=1 << 20),
        name="part",
    )(in_vmem(array))


def copies_body(in_ref, out_ref):
    for k in range(out_ref.shape[0]):
        out_ref[k] = in_ref[...]


def hidden_ring(hidden, up, down, count):
    half, rows = count // 2, hidden.shape[0]
    below, above = hidden, hidden
    sources = []
    for step in range(1, half + 1):
        if step == half:
            below, above = part(below, 0, rows // 2), part(above, rows // 2, rows // 2)
        below = lax.ppermute(below, "dp", up)
        above = lax.ppermute(above, "dp", down)
        if step < half:
            sources += [(-step, [below]), (step, [above])]
        else:
            sources.append((half, [below, above]))
    return sources


def reorder(me, offsets, slots_ref, rows_ref):
    count, per_source = slots_ref.shape[1], slots_ref.shape[0] * CAP
    for n, offset in enumerate(offsets):
        i = (me + offset) % count
        for j in range(slots_ref.shape[0]):
            at = n * per_source + j * CAP
            rows_ref[at : at + CAP, :] = slots_ref[j, i]


def products(hidden_ref, rows_ref):
    block = hidden_ref.shape[1] // 4
    for g in range(4):
        units = slice(g * block, (g + 1) * block)
        yield units, lax.dot_general(
            hidden_ref[:, units],
            rows_ref[...],
            (((0,), (0,)), ((), ())),
            preferred_element_type=jnp.float32,
        )


def first_body(offsets, where_ref, slots_ref, *rest):
    piece_refs, out_ref, hidden_ref, rows_ref = rest[:-3], *rest[-3:]
    reorder(where_ref[0], offsets, slots_ref, rows_ref)
    at = 0
    for ref in piece_refs:
        hidden_ref[at : at + ref.shape[0], :] = ref[...]
        at += ref.shape[0]
    for units, total in products(hidden_ref, rows_ref):
        out_ref[units, :] = total.astype(out_ref.dtype)


def second_body(offsets, where_ref, slots_ref, hidden_ref, done_ref, out_ref, rows_ref):
    width, core = slots_ref.shape[-1], where_ref[1]
    reorder(where_ref[0], offsets, slots_ref, rows_ref)
    out_ref[:, pl.ds(pl.multiple_of(core * width, 128), width)] = done_ref[...]
    column = pl.multiple_of((1 - core) * width, 128)
    for units, total in products(hidden_ref, rows_ref):
        out_ref[units, pl.ds(column, width)] = total.astype(out_ref.dtype)


def in_vmem(array):
    return pltpu.with_memory_space_constraint(array, pltpu.VMEM)


def local(grad_out, expert_ids, route_gates, saved_hidden):
    data_count = lax.axis_size("dp")
    expert_count = lax.axis_size("expert")
    tensor_count = lax.axis_size("tensor")
    chips = tensor_count // CORES
    width = grad_out.shape[1]
    hidden = saved_hidden[0]
    rows, units = hidden.shape
    y_up = [(k, (k + 1) % data_count) for k in range(data_count)]
    y_down = [(k, (k - 1) % data_count) for k in range(data_count)]
    swap = [(k, k ^ 1) for k in range(tensor_count)]
    same_core = [[c + CORES * k for k in range(chips)] for c in range(CORES)]
    smem = pl.BlockSpec(memory_space=pltpu.SMEM)
    vmem = pl.BlockSpec(memory_space=pltpu.VMEM)

    sources = [(0, [hidden])] + hidden_ring(hidden, y_up, y_down, data_count)

    slots = pl.pallas_call(
        lambda *refs: select_body(expert_count, *refs),
        out_shape=pltpu.VMEM((expert_count, CAP, width), jnp.bfloat16),
        name="select",
    )(expert_ids.T, route_gates.T, grad_out)
    slots = lax.all_to_all(slots, "expert", 0, 0, tiled=True)
    slots = lax.all_to_all(slots, "tensor", 0, 0, tiled=True, axis_index_groups=same_core)
    slots = lax.all_to_all(slots, "dp", 0, 0, tiled=True)
    copies = pl.pallas_call(
        copies_body,
        out_shape=jax.ShapeDtypeStruct((chips, *slots.shape), slots.dtype),
        in_specs=[vmem],
        out_specs=vmem,
        compiler_params=pltpu.CompilerParams(vmem_limit_bytes=4 << 20),
        name="copies",
    )(in_vmem(slots))
    mine = lax.all_to_all(copies, "tensor", 0, 0, tiled=False, axis_index_groups=same_core)
    other = lax.ppermute(mine, "tensor", swap)

    place = jnp.stack([lax.axis_index("dp"), lax.axis_index("tensor") % CORES])
    place = place.astype(jnp.int32)
    offsets = [offset for offset, _ in sources]
    pieces = [p if abs(o) == 1 else in_vmem(p) for o, ps in sources for p in ps]
    taken = data_count * rows
    params = pltpu.CompilerParams(vmem_limit_bytes=14 << 20)
    scratch = [pltpu.VMEM((taken, width), jnp.bfloat16)]
    done, gathered = pl.pallas_call(
        lambda *refs: first_body(offsets, *refs),
        out_shape=(
            pltpu.VMEM((units, width), jnp.bfloat16),
            pltpu.VMEM((taken, units), jnp.bfloat16),
        ),
        in_specs=[smem] + [vmem] * (1 + len(pieces)),
        out_specs=(vmem, vmem),
        scratch_shapes=scratch,
        compiler_params=params,
        name="first",
    )(place, in_vmem(mine), *pieces)
    out = pl.pallas_call(
        lambda *refs: second_body(offsets, *refs),
        out_shape=jax.ShapeDtypeStruct((units, CORES * width), jnp.bfloat16),
        in_specs=[smem] + [vmem] * 3,
        out_specs=vmem,
        scratch_shapes=scratch,
        compiler_params=params,
        name="second",
    )(place, in_vmem(other), in_vmem(gathered), in_vmem(done))
    return out[None]


def solution(mesh):
    in_specs = (
        P(("dp", "expert"), "tensor"),
        P(("dp", "expert"), None),
        P(("dp", "expert"), None),
        P("expert", "dp", "tensor"),
    )
    out_specs = P("expert", "tensor", "dp")

    return jax.shard_map(local, mesh=mesh, in_specs=in_specs, out_specs=out_specs, check_vma=False)
```

profile of v0, /device:TPU:1, one launch (start us, length us, event | category | flops | bytes accessed | tf_op | source)
XLA Modules:
  0.0 164.4 jit_solution(1003934249388593407)
XLA Ops:
  0.0 1.3 select.3
  1.3 26.0 %all_to_all.20 = bf16[8,32,384]{2,1,0:T(8,128)(2,1)S(1)} all-to-all(bf16[8,32,384]{2,1,0:T(8,128)(2,1)S(1)} %select.3), channel_id=1, replica_groups=mesh['dp'=8,'expert'=8,'tensor'=16] {'expert'}, dimensions={0} | all-to-all | bytes 393216 | tf_op jit(solution)/shard_map/all_to_all | solution.py:149
  27.3 15.0 %all_to_all.21 = bf16[8,32,384]{2,1,0:T(8,128)(2,1)S(1)} all-to-all(bf16[8,32,384]{2,1,0:T(8,128)(2,1)S(1)} %all_to_all.20), channel_id=1, replica_groups={{0,2,4,6,8,10,12,14},{1,3,5,7,9,11,13,15},{16,18,20,22,24,26,28,30},{17..., dimensions={0} | all-to-all | bytes 393216 | tf_op jit(solution)/shard_map/all_to_all | solution.py:150
  42.3 15.8 %all_to_all.22.in_ref = bf16[8,32,384]{2,1,0:T(8,128)(2,1)S(1)} all-to-all(bf16[8,32,384]{2,1,0:T(8,128)(2,1)S(1)} %all_to_all.21), channel_id=1, replica_groups=mesh['dp'=8,'expert'=8,'tensor'=16] {'dp'}, dimensions={0} | all-to-all | bytes 393216 | tf_op jit(solution)/shard_map/all_to_all | solution.py:151
  58.1 1.3 copies.1
  59.4 3.7 %all-to-all-start.3 = ((bf16[8,8,32,384]{3,2,1,0:T(8,128)(2,1)}), bf16[8,8,32,384]{3,2,1,0:T(8,128)(2,1)S(1)}, u32[]{:S(2)}, u32[]{:S(2)}) async-start(bf16[8,8,32,384]{3,2,1,0:T(8,128)(2,1)} %copies.1), calls=%async_computation.3 | async-start | bytes 3145728 | tf_op jit(solution)/shard_map/all_to_all | solution.py:160
  63.1 1.9 %collective-permute-start.2 = (bf16[256,1024]{1,0:T(8,128)(2,1)S(1)}, bf16[256,1024]{1,0:T(8,128)(2,1)S(1)}, u32[]{:S(2)}, u32[]{:S(2)}) collective-permute-start(bf16[256,1024]{1,0:T(8,128)(2,1)S(1)} %bitcast.6), channel_id=1, source_target_pairs={{0,896},{128,0},{256,128},{384,256},{512,384},{640,512},{768,640},... | collective-permute-start | bytes 1572872 | tf_op jit(solution)/shard_map/ppermute | solution.py:74
  65.0 3.4 %collective-permute-start.1 = (bf16[256,1024]{1,0:T(8,128)(2,1)S(1)}, bf16[256,1024]{1,0:T(8,128)(2,1)S(1)}, u32[]{:S(2)}, u32[]{:S(2)}) collective-permute-start(bf16[256,1024]{1,0:T(8,128)(2,1)S(1)} %bitcast.7), channel_id=1, source_target_pairs={{0,128},{128,256},{256,384},{384,512},{512,640},{640,768},{768,896... | collective-permute-start | bytes 1572872 | tf_op jit(solution)/shard_map/ppermute | solution.py:73
  68.4 31.7 %all-to-all-done.3.refs_1_ = bf16[8,8,32,384]{3,2,1,0:T(8,128)(2,1)S(1)} async-done(((bf16[8,8,32,384]{3,2,1,0:T(8,128)(2,1)}), bf16[8,8,32,384]{3,2,1,0:T(8,128)(2,1)S(1)}, u32[]{:S(2)}, u32[]{:S(2)}) %all-to-all-start.3) | async-done | bytes 1572896 | tf_op jit(solution)/shard_map/all_to_all | solution.py:160
  100.1 5.8 %collective-permute-start = (bf16[8,8,32,384]{3,2,1,0:T(8,128)(2,1)S(1)}, bf16[8,8,32,384]{3,2,1,0:T(8,128)(2,1)}, u32[]{:S(2)}, u32[]{:S(2)}) collective-permute-start(bf16[8,8,32,384]{3,2,1,0:T(8,128)(2,1)S(1)} %all-to-all-done.3.refs_1_), channel_id=1, source_target_pairs={{0,1},{1,0},{2,3},{3,2},{4,5},{5,4},{6,7},{7,6},{8,9},{9,8},{10,11... | collective-permute-start | bytes 4718600 | tf_op jit(solution)/shard_map/ppermute | solution.py:161
  105.9 1.9 %collective-permute-start.4 = (bf16[256,1024]{1,0:T(8,128)(2,1)S(1)}, bf16[256,1024]{1,0:T(8,128)(2,1)S(1)}, u32[]{:S(2)}, u32[]{:S(2)}) collective-permute-start(bf16[256,1024]{1,0:T(8,128)(2,1)S(1)} %collective-permute-done.2.refs_4_), channel_id=1, source_target_pairs={{0,896},{128,0},{256,128},{384,256},{512,384},{640,512},{768,640},... | collective-permute-start | bytes 1572872 | tf_op jit(solution)/shard_map/ppermute | solution.py:74
  108.6 3.4 %collective-permute-start.3 = (bf16[256,1024]{1,0:T(8,128)(2,1)S(1)}, bf16[256,1024]{1,0:T(8,128)(2,1)S(1)}, u32[]{:S(2)}, u32[]{:S(2)}) collective-permute-start(bf16[256,1024]{1,0:T(8,128)(2,1)S(1)} %collective-permute-done.1.refs_3_), channel_id=1, source_target_pairs={{0,128},{128,256},{256,384},{384,512},{512,640},{640,768},{768,896... | collective-permute-start | bytes 1572872 | tf_op jit(solution)/shard_map/ppermute | solution.py:73
  112.8 8.4 %collective-permute-done.4.refs_6_ = bf16[256,1024]{1,0:T(8,128)(2,1)S(1)} collective-permute-done((bf16[256,1024]{1,0:T(8,128)(2,1)S(1)}, bf16[256,1024]{1,0:T(8,128)(2,1)S(1)}, u32[]{:S(2)}, u32[]{:S(2)}) %collective-permute-start.4) | collective-permute-done | bytes 524320 | tf_op jit(solution)/shard_map/ppermute | solution.py:74
  121.3 3.4 %collective-permute-start.6 = (bf16[256,1024]{1,0:T(8,128)(2,1)S(1)}, bf16[256,1024]{1,0:T(8,128)(2,1)S(1)}, u32[]{:S(2)}, u32[]{:S(2)}) collective-permute-start(bf16[256,1024]{1,0:T(8,128)(2,1)S(1)} %collective-permute-done.4.refs_6_), channel_id=1, source_target_pairs={{0,896},{128,0},{256,128},{384,256},{512,384},{640,512},{768,640},... | collective-permute-start | bytes 1572872 | tf_op jit(solution)/shard_map/ppermute | solution.py:74
  125.2 1.9 %collective-permute-start.5 = (bf16[256,1024]{1,0:T(8,128)(2,1)S(1)}, bf16[256,1024]{1,0:T(8,128)(2,1)S(1)}, u32[]{:S(2)}, u32[]{:S(2)}) collective-permute-start(bf16[256,1024]{1,0:T(8,128)(2,1)S(1)} %collective-permute-done.3.refs_5_), channel_id=1, source_target_pairs={{0,128},{128,256},{256,384},{384,512},{512,640},{640,768},{768,896... | collective-permute-start | bytes 1572872 | tf_op jit(solution)/shard_map/ppermute | solution.py:73
  127.1 8.6 %collective-permute-done.6.refs_0_.refs_8_ = bf16[256,1024]{1,0:T(8,128)(2,1)S(1)} collective-permute-done((bf16[256,1024]{1,0:T(8,128)(2,1)S(1)}, bf16[256,1024]{1,0:T(8,128)(2,1)S(1)}, u32[]{:S(2)}, u32[]{:S(2)}) %collective-permute-start.6) | collective-permute-done | bytes 524320 | tf_op jit(solution)/shard_map/ppermute | solution.py:74
  136.5 4.9 %collective-permute-start.8 = (bf16[128,1024]{1,0:T(8,128)(2,1)}, bf16[128,1024]{1,0:T(8,128)(2,1)S(1)}, u32[]{:S(2)}, u32[]{:S(2)}) collective-permute-start(bf16[128,1024]{1,0:T(8,128)(2,1)} %part.3), channel_id=1, source_target_pairs={{0,896},{128,0},{256,128},{384,256},{512,384},{640,512},{768,640},... | collective-permute-start | bytes 786440 | tf_op jit(solution)/shard_map/ppermute | solution.py:74
  142.1 1.9 %collective-permute-start.7 = (bf16[128,1024]{1,0:T(8,128)(2,1)}, bf16[128,1024]{1,0:T(8,128)(2,1)}, u32[]{:S(2)}, u32[]{:S(2)}) collective-permute-start(bf16[128,1024]{1,0:T(8,128)(2,1)} %part.2), channel_id=1, source_target_pairs={{0,128},{128,256},{256,384},{384,512},{512,640},{640,768},{768,896... | collective-permute-start | bytes 786440 | tf_op jit(solution)/shard_map/ppermute | solution.py:73
  144.1 1.8 %collective-permute-done.8.refs_10_ = bf16[128,1024]{1,0:T(8,128)(2,1)S(1)} collective-permute-done((bf16[128,1024]{1,0:T(8,128)(2,1)}, bf16[128,1024]{1,0:T(8,128)(2,1)S(1)}, u32[]{:S(2)}, u32[]{:S(2)}) %collective-permute-start.8) | collective-permute-done | bytes 262176 | tf_op jit(solution)/shard_map/ppermute | solution.py:74
  145.9 5.8 %collective-permute-done.7.refs_9_ = bf16[128,1024]{1,0:T(8,128)(2,1)} collective-permute-done((bf16[128,1024]{1,0:T(8,128)(2,1)}, bf16[128,1024]{1,0:T(8,128)(2,1)}, u32[]{:S(2)}, u32[]{:S(2)}) %collective-permute-start.7) | collective-permute-done | bytes 262176 | tf_op jit(solution)/shard_map/ppermute | solution.py:73
  151.7 1.0 copy-done.2
  153.7 1.0 copy-done.6
  155.8 3.5 %first.1 = (bf16[1024,384]{1,0:T(8,128)(2,1)S(1)}, bf16[2048,1024]{1,0:T(8,128)(2,1)S(1)}) custom-call(s32[2]{0:T(128)S(1)} %pad_add_fusion.refs_0_, bf16[8,8,32,384]{3,2,1,0:T(8,128)(2,1)S(1)} %all-to-all-done.3.refs_1_, bf16[256,1024]{1,0:T(8,128)(2,1)S(1)} %bitcast.8, bf16[256,1024]{1,0:T(8,128)(2,1)S(1)} %copy-done.4, bf16[256,1024]{1,0:T(8,128)(2,1)S(1)} %copy-done.2, ...), custom_call_target="tpu_custom_call" | custom-call | tf_op jit(solution)/shard_map/first/pallas_call | solution.py:170
  159.3 5.1 %second.1 = bf16[1024,768]{1,0:T(8,128)(2,1)} custom-call(s32[2]{0:T(128)S(1)} %pad_add_fusion.refs_0_, bf16[8,8,32,384]{3,2,1,0:T(8,128)(2,1)} %collective-permute-done.refs_1_, bf16[2048,1024]{1,0:T(8,128)(2,1)S(1)} %get-tuple-element.7.refs_2_, bf16[1024,384]{1,0:T(8,128)(2,1)S(1)} %get-tuple-element.8.refs_3_), custom_call_target="tpu_custom_call" | custom-call | tf_op jit(solution)/shard_map/second/pallas_call | solution.py:182
  (24 shorter events, 5.8 us)
Async XLA Ops:
  59.4 3.7 %copy-start = (bf16[1,256,1024]{2,1,0:T(8,128)(2,1)S(1)}, bf16[1,256,1024]{2,1,0:T(8,128)(2,1)}, u32[]{:S(2)}) copy-start(bf16[1,256,1024]{2,1,0:T(8,128)(2,1)} %param.7) | copy-start | bytes 1572868
  59.4 40.7 %all-to-all-start.3 = ((bf16[8,8,32,384]{3,2,1,0:T(8,128)(2,1)}), bf16[8,8,32,384]{3,2,1,0:T(8,128)(2,1)S(1)}, u32[]{:S(2)}, u32[]{:S(2)}) async-start(bf16[8,8,32,384]{3,2,1,0:T(8,128)(2,1)} %copies.1), calls=%async_computation.3 | async-start | bytes 3145728 | tf_op jit(solution)/shard_map/all_to_all | solution.py:160
  63.1 42.8 %collective-permute-start.2 = (bf16[256,1024]{1,0:T(8,128)(2,1)S(1)}, bf16[256,1024]{1,0:T(8,128)(2,1)S(1)}, u32[]{:S(2)}, u32[]{:S(2)}) collective-permute-start(bf16[256,1024]{1,0:T(8,128)(2,1)S(1)} %bitcast.6), channel_id=1, source_target_pairs={{0,896},{128,0},{256,128},{384,256},{512,384},{640,512},{768,640},... | collective-permute-start | bytes 1572872 | tf_op jit(solution)/shard_map/ppermute | solution.py:74
  65.0 43.6 %collective-permute-start.1 = (bf16[256,1024]{1,0:T(8,128)(2,1)S(1)}, bf16[256,1024]{1,0:T(8,128)(2,1)S(1)}, u32[]{:S(2)}, u32[]{:S(2)}) collective-permute-start(bf16[256,1024]{1,0:T(8,128)(2,1)S(1)} %bitcast.7), channel_id=1, source_target_pairs={{0,128},{128,256},{256,384},{384,512},{512,640},{640,768},{768,896... | collective-permute-start | bytes 1572872 | tf_op jit(solution)/shard_map/ppermute | solution.py:73
  100.1 59.2 %collective-permute-start = (bf16[8,8,32,384]{3,2,1,0:T(8,128)(2,1)S(1)}, bf16[8,8,32,384]{3,2,1,0:T(8,128)(2,1)}, u32[]{:S(2)}, u32[]{:S(2)}) collective-permute-start(bf16[8,8,32,384]{3,2,1,0:T(8,128)(2,1)S(1)} %all-to-all-done.3.refs_1_), channel_id=1, source_target_pairs={{0,1},{1,0},{2,3},{3,2},{4,5},{5,4},{6,7},{7,6},{8,9},{9,8},{10,11... | collective-permute-start | bytes 4718600 | tf_op jit(solution)/shard_map/ppermute | solution.py:161
  105.9 15.4 %collective-permute-start.4 = (bf16[256,1024]{1,0:T(8,128)(2,1)S(1)}, bf16[256,1024]{1,0:T(8,128)(2,1)S(1)}, u32[]{:S(2)}, u32[]{:S(2)}) collective-permute-start(bf16[256,1024]{1,0:T(8,128)(2,1)S(1)} %collective-permute-done.2.refs_4_), channel_id=1, source_target_pairs={{0,896},{128,0},{256,128},{384,256},{512,384},{640,512},{768,640},... | collective-permute-start | bytes 1572872 | tf_op jit(solution)/shard_map/ppermute | solution.py:74
  107.8 0.8 copy-start.1
  108.6 16.6 %collective-permute-start.3 = (bf16[256,1024]{1,0:T(8,128)(2,1)S(1)}, bf16[256,1024]{1,0:T(8,128)(2,1)S(1)}, u32[]{:S(2)}, u32[]{:S(2)}) collective-permute-start(bf16[256,1024]{1,0:T(8,128)(2,1)S(1)} %collective-permute-done.1.refs_3_), channel_id=1, source_target_pairs={{0,128},{128,256},{256,384},{384,512},{512,640},{640,768},{768,896... | collective-permute-start | bytes 1572872 | tf_op jit(solution)/shard_map/ppermute | solution.py:73
  112.0 0.8 copy-start.3
  121.3 20.1 %copy-start.5 = (bf16[256,1024]{1,0:T(8,128)(2,1)}, bf16[256,1024]{1,0:T(8,128)(2,1)S(1)}, u32[]{:S(2)}) copy-start(bf16[256,1024]{1,0:T(8,128)(2,1)S(1)} %collective-permute-done.4.refs_6_) | copy-start | bytes 1572868
  121.3 14.5 %collective-permute-start.6 = (bf16[256,1024]{1,0:T(8,128)(2,1)S(1)}, bf16[256,1024]{1,0:T(8,128)(2,1)S(1)}, u32[]{:S(2)}, u32[]{:S(2)}) collective-permute-start(bf16[256,1024]{1,0:T(8,128)(2,1)S(1)} %collective-permute-done.4.refs_6_), channel_id=1, source_target_pairs={{0,896},{128,0},{256,128},{384,256},{512,384},{640,512},{768,640},... | collective-permute-start | bytes 1572872 | tf_op jit(solution)/shard_map/ppermute | solution.py:74
  125.2 16.9 %copy-start.7 = (bf16[256,1024]{1,0:T(8,128)(2,1)}, bf16[256,1024]{1,0:T(8,128)(2,1)S(1)}, u32[]{:S(2)}) copy-start(bf16[256,1024]{1,0:T(8,128)(2,1)S(1)} %collective-permute-done.3.refs_5_) | copy-start | bytes 1572868
  125.2 16.2 %collective-permute-start.5 = (bf16[256,1024]{1,0:T(8,128)(2,1)S(1)}, bf16[256,1024]{1,0:T(8,128)(2,1)S(1)}, u32[]{:S(2)}, u32[]{:S(2)}) collective-permute-start(bf16[256,1024]{1,0:T(8,128)(2,1)S(1)} %collective-permute-done.3.refs_5_), channel_id=1, source_target_pairs={{0,128},{128,256},{256,384},{384,512},{512,640},{640,768},{768,896... | collective-permute-start | bytes 1572872 | tf_op jit(solution)/shard_map/ppermute | solution.py:73
  136.5 9.4 %collective-permute-start.8 = (bf16[128,1024]{1,0:T(8,128)(2,1)}, bf16[128,1024]{1,0:T(8,128)(2,1)S(1)}, u32[]{:S(2)}, u32[]{:S(2)}) collective-permute-start(bf16[128,1024]{1,0:T(8,128)(2,1)} %part.3), channel_id=1, source_target_pairs={{0,896},{128,0},{256,128},{384,256},{512,384},{640,512},{768,640},... | collective-permute-start | bytes 786440 | tf_op jit(solution)/shard_map/ppermute | solution.py:74
  142.1 9.5 %collective-permute-start.7 = (bf16[128,1024]{1,0:T(8,128)(2,1)}, bf16[128,1024]{1,0:T(8,128)(2,1)}, u32[]{:S(2)}, u32[]{:S(2)}) collective-permute-start(bf16[128,1024]{1,0:T(8,128)(2,1)} %part.2), channel_id=1, source_target_pairs={{0,128},{128,256},{256,384},{384,512},{512,640},{640,768},{768,896... | collective-permute-start | bytes 786440 | tf_op jit(solution)/shard_map/ppermute | solution.py:73
  151.6 1.0 copy-start.2
  152.7 1.0 copy-start.4
  153.7 1.0 copy-start.6
  154.8 1.0 copy-start.8
where the time goes:
time: 165 us; the launch traced here: 164 us
  waiting for transfers between devices  56.9 us (34%)
  blocking collectives  56.8 us (34%)
  starting transfers between devices  32.1 us (19%)
  Pallas kernels  12.6 us (8%)
  local copies, waits for them, and re-layouts  5.78 us (4%)
    all_to_all x1, waiting for transfers between devices, local(): lax.all_to_all(copies, 'tensor', 0, 0, tiled=False, axis_index_groups=sam...  31.7 us
    all_to_all x1, blocking collectives, local(): slots = lax.all_to_all(slots, 'expert', 0, 0, tiled=True)  26 us
    ppermute x4, waiting for transfers between devices, hidden_ring(): above = lax.ppermute(above, 'dp', down)  18.8 us
    all_to_all x1, blocking collectives, local(): slots = lax.all_to_all(slots, 'dp', 0, 0, tiled=True)  15.8 us
    all_to_all x1, blocking collectives, local(): lax.all_to_all(slots, 'tensor', 0, 0, tiled=True, axis_index_groups=same_...  15 us
    ppermute x4, starting transfers between devices, hidden_ring(): above = lax.ppermute(above, 'dp', down)  12.1 us
    ppermute x4, starting transfers between devices, hidden_ring(): below = lax.ppermute(below, 'dp', up)  10.5 us
    ppermute x4, waiting for transfers between devices, hidden_ring(): below = lax.ppermute(below, 'dp', up)  6.33 us
  transfers between devices with their start and end apart: 10, of which 6 were waited for; matrix products, arithmetic and copies ran while one was open for 0% of the time, Pallas kernels for 3%

commit v1 on v0

--- a/solution.py
+++ b/solution.py
@@ -42,34 +42,38 @@
         out_ref[e] = (picked * weight).astype(out_ref.dtype)
 
 
-def part_body(at, in_ref, out_ref):
-    out_ref[...] = in_ref[at : at + out_ref.shape[0], :]
-
-
-def part(array, at, size):
+def parts_body(in_ref, *out_refs):
+    at = 0
+    for ref in out_refs:
+        ref[...] = in_ref[at : at + ref.shape[0]]
+        at += ref.shape[0]
+
+
+def two_halves(array):
     vmem = pl.BlockSpec(memory_space=pltpu.VMEM)
+    half = pltpu.VMEM((array.shape[0] // 2, *array.shape[1:]), array.dtype)
     return pl.pallas_call(
-        lambda *refs: part_body(at, *refs),
-        out_shape=pltpu.VMEM((size, array.shape[1]), array.dtype),
+        parts_body,
+        out_shape=(half, half),
         in_specs=[vmem],
-        out_specs=vmem,
-        compiler_params=pltpu.CompilerParams(vmem_limit_bytes=1 << 20),
-        name="part",
+        out_specs=(vmem, vmem),
+        compiler_params=pltpu.CompilerParams(vmem_limit_bytes=2 << 20),
+        name="halves",
     )(in_vmem(array))
 
 
-def copies_body(in_ref, out_ref):
-    for k in range(out_ref.shape[0]):
+def twice_body(in_ref, out_ref):
+    for k in range(2):
         out_ref[k] = in_ref[...]
 
 
 def hidden_ring(hidden, up, down, count):
-    half, rows = count // 2, hidden.shape[0]
+    half = count // 2
     below, above = hidden, hidden
     sources = []
     for step in range(1, half + 1):
         if step == half:
-            below, above = part(below, 0, rows // 2), part(above, rows // 2, rows // 2)
+            below, above = two_halves(below)[0], two_halves(above)[1]
         below = lax.ppermute(below, "dp", up)
         above = lax.ppermute(above, "dp", down)
         if step < half:
@@ -79,13 +83,26 @@
     return sources
 
 
-def reorder(me, offsets, slots_ref, rows_ref):
-    count, per_source = slots_ref.shape[1], slots_ref.shape[0] * CAP
-    for n, offset in enumerate(offsets):
-        i = (me + offset) % count
-        for j in range(slots_ref.shape[0]):
-            at = n * per_source + j * CAP
-            rows_ref[at : at + CAP, :] = slots_ref[j, i]
+def assemble_body(count, where_ref, *refs):
+    me, mine = where_ref[0], where_ref[1]
+    own_ref, below_ref, above_ref, *far_refs, out_ref = refs
+    groups = count // 2
+    size = own_ref.shape[1] * own_ref.shape[2]
+    for step, pieces in ((0, [own_ref]), (-1, [below_ref]), (1, [above_ref]), (2, far_refs)):
+        row = ((mine + step) % groups) * size
+        i = 0
+        for ref in pieces:
+            for k in range(ref.shape[0]):
+                ahead = (i - me) % count
+                place = jnp.where(
+                    ahead <= count // 2,
+                    2 * ahead - jnp.where(ahead == count // 2, 1, 0),
+                    2 * (count - ahead) - 1,
+                )
+                for part in range(ref.shape[1]):
+                    start = place * (groups * size) + row + part * CAP
+                    out_ref[pl.ds(pl.multiple_of(start, CAP), CAP), :] = ref[k, part]
+                i += 1
 
 
 def products(hidden_ref, rows_ref):
@@ -100,9 +117,8 @@
         )
 
 
-def first_body(offsets, where_ref, slots_ref, *rest):
-    piece_refs, out_ref, hidden_ref, rows_ref = rest[:-3], *rest[-3:]
-    reorder(where_ref[0], offsets, slots_ref, rows_ref)
+def first_body(rows_ref, *rest):
+    piece_refs, out_ref, hidden_ref = rest[:-2], *rest[-2:]
     at = 0
     for ref in piece_refs:
         hidden_ref[at : at + ref.shape[0], :] = ref[...]
@@ -111,9 +127,8 @@
         out_ref[units, :] = total.astype(out_ref.dtype)
 
 
-def second_body(offsets, where_ref, slots_ref, hidden_ref, done_ref, out_ref, rows_ref):
-    width, core = slots_ref.shape[-1], where_ref[1]
-    reorder(where_ref[0], offsets, slots_ref, rows_ref)
+def second_body(where_ref, rows_ref, hidden_ref, done_ref, out_ref):
+    width, core = rows_ref.shape[-1], where_ref[2]
     out_ref[:, pl.ds(pl.multiple_of(core * width, 128), width)] = done_ref[...]
     column = pl.multiple_of((1 - core) * width, 128)
     for units, total in products(hidden_ref, rows_ref):
@@ -134,6 +149,10 @@
     rows, units = hidden.shape
     y_up = [(k, (k + 1) % data_count) for k in range(data_count)]
     y_down = [(k, (k - 1) % data_count) for k in range(data_count)]
+
+    def shift(by):
+        return [(k, (k + by) % tensor_count) for k in range(tensor_count)]
+
     swap = [(k, k ^ 1) for k in range(tensor_count)]
     same_core = [[c + CORES * k for k in range(chips)] for c in range(CORES)]
     smem = pl.BlockSpec(memory_space=pltpu.SMEM)
@@ -147,44 +166,55 @@
         name="select",
     )(expert_ids.T, route_gates.T, grad_out)
     slots = lax.all_to_all(slots, "expert", 0, 0, tiled=True)
+    groups = chips // 2
+    slots = pl.pallas_call(
+        twice_body,
+        out_shape=jax.ShapeDtypeStruct((2, *slots.shape), slots.dtype),
+        in_specs=[vmem],
+        out_specs=vmem,
+        compiler_params=pltpu.CompilerParams(vmem_limit_bytes=2 << 20),
+        name="twice",
+    )(in_vmem(slots))
+    slots = slots.reshape(chips, expert_count // groups, CAP, width)
     slots = lax.all_to_all(slots, "tensor", 0, 0, tiled=True, axis_index_groups=same_core)
     slots = lax.all_to_all(slots, "dp", 0, 0, tiled=True)
-    copies = pl.pallas_call(
-        copies_body,
-        out_shape=jax.ShapeDtypeStruct((chips, *slots.shape), slots.dtype),
-        in_specs=[vmem],
+    lower, upper = two_halves(slots)
+    below = lax.ppermute(slots, "tensor", shift(CORES))
+    above = lax.ppermute(slots, "tensor", shift(-CORES))
+    lower = lax.ppermute(lower, "tensor", shift(2 * CORES))
+    upper = lax.ppermute(upper, "tensor", shift(-2 * CORES))
+
+    t = lax.axis_index("tensor")
+    place = jnp.stack([lax.axis_index("dp"), t // CORES % groups, t % CORES]).astype(jnp.int32)
+    taken = data_count * rows
+    mine = pl.pallas_call(
+        lambda *refs: assemble_body(data_count, *refs),
+        out_shape=pltpu.VMEM((taken, width), jnp.bfloat16),
+        in_specs=[smem] + [vmem] * 5,
         out_specs=vmem,
         compiler_params=pltpu.CompilerParams(vmem_limit_bytes=4 << 20),
-        name="copies",
-    )(in_vmem(slots))
-    mine = lax.all_to_all(copies, "tensor", 0, 0, tiled=False, axis_index_groups=same_core)
+        name="assemble",
+    )(place, *[in_vmem(p) for p in (slots, below, above, lower, upper)])
     other = lax.ppermute(mine, "tensor", swap)
 
-    place = jnp.stack([lax.axis_index("dp"), lax.axis_index("tensor") % CORES])
-    place = place.astype(jnp.int32)
-    offsets = [offset for offset, _ in sources]
-    pieces = [p if abs(o) == 1 else in_vmem(p) for o, ps in sources for p in ps]
-    taken = data_count * rows
+    pieces = [p for _, ps in sources for p in ps]
     params = pltpu.CompilerParams(vmem_limit_bytes=14 << 20)
-    scratch = [pltpu.VMEM((taken, width), jnp.bfloat16)]
     done, gathered = pl.pallas_call(
-        lambda *refs: first_body(offsets, *refs),
+        first_body,
         out_shape=(
             pltpu.VMEM((units, width), jnp.bfloat16),
             pltpu.VMEM((taken, units), jnp.bfloat16),
         ),
-        in_specs=[smem] + [vmem] * (1 + len(pieces)),
+        in_specs=[vmem] * (1 + len(pieces)),
         out_specs=(vmem, vmem),
-        scratch_shapes=scratch,
         compiler_params=params,
         name="first",
-    )(place, in_vmem(mine), *pieces)
+    )(in_vmem(mine), *pieces)
     out = pl.pallas_call(
-        lambda *refs: second_body(offsets, *refs),
+        second_body,
         out_shape=jax.ShapeDtypeStruct((units, CORES * width), jnp.bfloat16),
         in_specs=[smem] + [vmem] * 3,
         out_specs=vmem,
-        scratch_shapes=scratch,
         compiler_params=params,
         name="second",
     )(place, in_vmem(other), in_vmem(gathered), in_vmem(done))

time: 165 us -> 152 us (0.921)
  the two profiles are of different devices: /device:TPU:1 before, /device:TPU:14 now
where the time goes in v1:
time: 152 us; the launch traced here: 151 us
  blocking collectives  62.5 us (41%)
  starting transfers between devices  42 us (28%)
  waiting for transfers between devices  36.3 us (24%)
  Pallas kernels  10.3 us (7%)
    all_to_all x1, blocking collectives, local(): slots = lax.all_to_all(slots, 'expert', 0, 0, tiled=True)  27 us
    ppermute x4, waiting for transfers between devices, hidden_ring(): above = lax.ppermute(above, 'dp', down)  21.2 us
    all_to_all x1, blocking collectives, local(): slots = lax.all_to_all(slots, 'dp', 0, 0, tiled=True)  19.2 us
    all_to_all x1, blocking collectives, local(): lax.all_to_all(slots, 'tensor', 0, 0, tiled=True, axis_index_groups=same_...  16.3 us
    ppermute x4, starting transfers between devices, hidden_ring(): above = lax.ppermute(above, 'dp', down)  15.5 us
    ppermute x4, starting transfers between devices, hidden_ring(): below = lax.ppermute(below, 'dp', up)  10.2 us
    ppermute x1, waiting for transfers between devices, local(): upper = lax.ppermute(upper, 'tensor', shift(-2 * CORES))  9.03 us
    ppermute x4, waiting for transfers between devices, hidden_ring(): below = lax.ppermute(below, 'dp', up)  6.07 us
  transfers between devices with their start and end apart: 13, of which 5 were waited for; matrix products, arithmetic and copies ran while one was open for 0% of the time, Pallas kernels for 3%

profile of v1, /device:TPU:14, one launch (start us, length us, event | category | flops | bytes accessed | tf_op | source)
XLA Modules:
  0.0 151.4 jit_solution(9716857163433410655)
XLA Ops:
  0.0 1.4 select.9
  1.4 27.0 %all_to_all.15.in_ref = bf16[8,32,384]{2,1,0:T(8,128)(2,1)S(1)} all-to-all(bf16[8,32,384]{2,1,0:T(8,128)(2,1)S(1)} %select.9), channel_id=1, replica_groups=mesh['dp'=8,'expert'=8,'tensor'=16] {'expert'}, dimensions={0} | all-to-all | bytes 393216 | tf_op jit(solution)/shard_map/all_to_all | solution.py:168
  28.4 16.3 %all_to_all.16 = bf16[8,2,32,384]{3,2,1,0:T(8,128)(2,1)S(1)} all-to-all(bf16[8,2,32,384]{3,2,1,0:T(8,128)(2,1)S(1)} %bitcast.8), channel_id=1, replica_groups={{0,2,4,6,8,10,12,14},{1,3,5,7,9,11,13,15},{16,18,20,22,24,26,28,30},{17..., dimensions={0} | all-to-all | bytes 786432 | tf_op jit(solution)/shard_map/all_to_all | solution.py:179
  44.7 19.2 %all_to_all.17.in_ref.refs_1_ = bf16[8,2,32,384]{3,2,1,0:T(8,128)(2,1)S(1)} all-to-all(bf16[8,2,32,384]{3,2,1,0:T(8,128)(2,1)S(1)} %all_to_all.16), channel_id=1, replica_groups=mesh['dp'=8,'expert'=8,'tensor'=16] {'dp'}, dimensions={0} | all-to-all | bytes 786432 | tf_op jit(solution)/shard_map/all_to_all | solution.py:180
  64.0 5.4 %collective-permute-start.2 = (bf16[4,2,32,384]{3,2,1,0:T(8,128)(2,1)S(1)}, bf16[4,2,32,384]{3,2,1,0:T(8,128)(2,1)S(1)}, u32[]{:S(2)}, u32[]{:S(2)}) collective-permute-start(bf16[4,2,32,384]{3,2,1,0:T(8,128)(2,1)S(1)} %get-tuple-element.11), channel_id=1, source_target_pairs={{0,4},{1,5},{2,6},{3,7},{4,8},{5,9},{6,10},{7,11},{8,12},{9,13},{1... | collective-permute-start | bytes 589832 | tf_op jit(solution)/shard_map/ppermute | solution.py:184
  69.4 3.4 %collective-permute-start.1 = (bf16[8,2,32,384]{3,2,1,0:T(8,128)(2,1)S(1)}, bf16[8,2,32,384]{3,2,1,0:T(8,128)(2,1)S(1)}, u32[]{:S(2)}, u32[]{:S(2)}) collective-permute-start(bf16[8,2,32,384]{3,2,1,0:T(8,128)(2,1)S(1)} %all_to_all.17.in_ref.refs_1_), channel_id=1, source_target_pairs={{0,14},{1,15},{2,0},{3,1},{4,2},{5,3},{6,4},{7,5},{8,6},{9,7},{10,... | collective-permute-start | bytes 1179656 | tf_op jit(solution)/shard_map/ppermute | solution.py:183
  72.8 3.7 %collective-permute-start = (bf16[8,2,32,384]{3,2,1,0:T(8,128)(2,1)S(1)}, bf16[8,2,32,384]{3,2,1,0:T(8,128)(2,1)S(1)}, u32[]{:S(2)}, u32[]{:S(2)}) collective-permute-start(bf16[8,2,32,384]{3,2,1,0:T(8,128)(2,1)S(1)} %all_to_all.17.in_ref.refs_1_), channel_id=1, source_target_pairs={{0,2},{1,3},{2,4},{3,5},{4,6},{5,7},{6,8},{7,9},{8,10},{9,11},{10,... | collective-permute-start | bytes 1179656 | tf_op jit(solution)/shard_map/ppermute | solution.py:182
  76.5 1.9 %collective-permute-start.6 = (bf16[256,1024]{1,0:T(8,128)(2,1)S(1)}, bf16[256,1024]{1,0:T(8,128)(2,1)S(1)}, u32[]{:S(2)}, u32[]{:S(2)}) collective-permute-start(bf16[256,1024]{1,0:T(8,128)(2,1)S(1)} %bitcast.9), channel_id=1, source_target_pairs={{0,896},{128,0},{256,128},{384,256},{512,384},{640,512},{768,640},... | collective-permute-start | bytes 1572872 | tf_op jit(solution)/shard_map/ppermute | solution.py:78
  78.4 3.9 %collective-permute-start.5 = (bf16[256,1024]{1,0:T(8,128)(2,1)S(1)}, bf16[256,1024]{1,0:T(8,128)(2,1)S(1)}, u32[]{:S(2)}, u32[]{:S(2)}) collective-permute-start(bf16[256,1024]{1,0:T(8,128)(2,1)S(1)} %bitcast.10), channel_id=1, source_target_pairs={{0,128},{128,256},{256,384},{384,512},{512,640},{640,768},{768,896... | collective-permute-start | bytes 1572872 | tf_op jit(solution)/shard_map/ppermute | solution.py:77
  82.3 1.9 %collective-permute-start.3 = (bf16[4,2,32,384]{3,2,1,0:T(8,128)(2,1)S(1)}, bf16[4,2,32,384]{3,2,1,0:T(8,128)(2,1)S(1)}, u32[]{:S(2)}, u32[]{:S(2)}) collective-permute-start(bf16[4,2,32,384]{3,2,1,0:T(8,128)(2,1)S(1)} %get-tuple-element.12), channel_id=1, source_target_pairs={{0,12},{1,13},{2,14},{3,15},{4,0},{5,1},{6,2},{7,3},{8,4},{9,5},{1... | collective-permute-start | bytes 589832 | tf_op jit(solution)/shard_map/ppermute | solution.py:185
  84.4 9.0 %collective-permute-done.3.refs_5_ = bf16[4,2,32,384]{3,2,1,0:T(8,128)(2,1)S(1)} collective-permute-done((bf16[4,2,32,384]{3,2,1,0:T(8,128)(2,1)S(1)}, bf16[4,2,32,384]{3,2,1,0:T(8,128)(2,1)S(1)}, u32[]{:S(2)}, u32[]{:S(2)}) %collective-permute-start.3) | collective-permute-done | bytes 196640 | tf_op jit(solution)/shard_map/ppermute | solution.py:185
  94.1 1.9 %collective-permute-start.4 = (bf16[2048,384]{1,0:T(8,128)(2,1)S(1)}, bf16[2048,384]{1,0:T(8,128)(2,1)S(1)}, u32[]{:S(2)}, u32[]{:S(2)}) collective-permute-start(bf16[2048,384]{1,0:T(8,128)(2,1)S(1)} %assemble.1.rows_ref), channel_id=1, source_target_pairs={{0,1},{1,0},{2,3},{3,2},{4,5},{5,4},{6,7},{7,6},{8,9},{9,8},{10,11... | collective-permute-start | bytes 4718600 | tf_op jit(solution)/shard_map/ppermute | solution.py:198
  96.1 3.4 %collective-permute-start.8 = (bf16[256,1024]{1,0:T(8,128)(2,1)S(1)}, bf16[256,1024]{1,0:T(8,128)(2,1)S(1)}, u32[]{:S(2)}, u32[]{:S(2)}) collective-permute-start(bf16[256,1024]{1,0:T(8,128)(2,1)S(1)} %collective-permute-done.6.rest_2_), channel_id=1, source_target_pairs={{0,896},{128,0},{256,128},{384,256},{512,384},{640,512},{768,640},... | collective-permute-start | bytes 1572872 | tf_op jit(solution)/shard_map/ppermute | solution.py:78
  99.5 2.4 %collective-permute-start.7 = (bf16[256,1024]{1,0:T(8,128)(2,1)S(1)}, bf16[256,1024]{1,0:T(8,128)(2,1)S(1)}, u32[]{:S(2)}, u32[]{:S(2)}) collective-permute-start(bf16[256,1024]{1,0:T(8,128)(2,1)S(1)} %collective-permute-done.5.rest_1_), channel_id=1, source_target_pairs={{0,128},{128,256},{256,384},{384,512},{512,640},{640,768},{768,896... | collective-permute-start | bytes 1572872 | tf_op jit(solution)/shard_map/ppermute | solution.py:77
  101.9 10.4 %collective-permute-done.8.rest_4_ = bf16[256,1024]{1,0:T(8,128)(2,1)S(1)} collective-permute-done((bf16[256,1024]{1,0:T(8,128)(2,1)S(1)}, bf16[256,1024]{1,0:T(8,128)(2,1)S(1)}, u32[]{:S(2)}, u32[]{:S(2)}) %collective-permute-start.8) | collective-permute-done | bytes 524320 | tf_op jit(solution)/shard_map/ppermute | solution.py:78
  112.3 4.6 %collective-permute-start.10 = (bf16[256,1024]{1,0:T(8,128)(2,1)S(1)}, bf16[256,1024]{1,0:T(8,128)(2,1)S(1)}, u32[]{:S(2)}, u32[]{:S(2)}) collective-permute-start(bf16[256,1024]{1,0:T(8,128)(2,1)S(1)} %collective-permute-done.8.rest_4_), channel_id=1, source_target_pairs={{0,896},{128,0},{256,128},{384,256},{512,384},{640,512},{768,640},... | collective-permute-start | bytes 1572872 | tf_op jit(solution)/shard_map/ppermute | solution.py:78
  116.9 1.9 %collective-permute-start.9 = (bf16[256,1024]{1,0:T(8,128)(2,1)S(1)}, bf16[256,1024]{1,0:T(8,128)(2,1)S(1)}, u32[]{:S(2)}, u32[]{:S(2)}) collective-permute-start(bf16[256,1024]{1,0:T(8,128)(2,1)S(1)} %collective-permute-done.7.rest_3_), channel_id=1, source_target_pairs={{0,128},{128,256},{256,384},{384,512},{512,640},{640,768},{768,896... | collective-permute-start | bytes 1572872 | tf_op jit(solution)/shard_map/ppermute | solution.py:77
  118.9 9.0 %collective-permute-done.10.in_ref.rest_6_ = bf16[256,1024]{1,0:T(8,128)(2,1)S(1)} collective-permute-done((bf16[256,1024]{1,0:T(8,128)(2,1)S(1)}, bf16[256,1024]{1,0:T(8,128)(2,1)S(1)}, u32[]{:S(2)}, u32[]{:S(2)}) %collective-permute-start.10) | collective-permute-done | bytes 524320 | tf_op jit(solution)/shard_map/ppermute | solution.py:78
  128.6 5.6 %collective-permute-start.12 = (bf16[128,1024]{1,0:T(8,128)(2,1)S(1)}, bf16[128,1024]{1,0:T(8,128)(2,1)S(1)}, u32[]{:S(2)}, u32[]{:S(2)}) collective-permute-start(bf16[128,1024]{1,0:T(8,128)(2,1)S(1)} %get-tuple-element.14), channel_id=1, source_target_pairs={{0,896},{128,0},{256,128},{384,256},{512,384},{640,512},{768,640},... | collective-permute-start | bytes 786440 | tf_op jit(solution)/shard_map/ppermute | solution.py:78
  135.0 1.9 %collective-permute-start.11 = (bf16[128,1024]{1,0:T(8,128)(2,1)S(1)}, bf16[128,1024]{1,0:T(8,128)(2,1)S(1)}, u32[]{:S(2)}, u32[]{:S(2)}) collective-permute-start(bf16[128,1024]{1,0:T(8,128)(2,1)S(1)} %get-tuple-element.13), channel_id=1, source_target_pairs={{0,128},{128,256},{256,384},{384,512},{512,640},{640,768},{768,896... | collective-permute-start | bytes 786440 | tf_op jit(solution)/shard_map/ppermute | solution.py:77
  136.9 1.8 %collective-permute-done.12.rest_8_ = bf16[128,1024]{1,0:T(8,128)(2,1)S(1)} collective-permute-done((bf16[128,1024]{1,0:T(8,128)(2,1)S(1)}, bf16[128,1024]{1,0:T(8,128)(2,1)S(1)}, u32[]{:S(2)}, u32[]{:S(2)}) %collective-permute-start.12) | collective-permute-done | bytes 262176 | tf_op jit(solution)/shard_map/ppermute | solution.py:78
  138.7 6.1 %collective-permute-done.11.rest_7_ = bf16[128,1024]{1,0:T(8,128)(2,1)S(1)} collective-permute-done((bf16[128,1024]{1,0:T(8,128)(2,1)S(1)}, bf16[128,1024]{1,0:T(8,128)(2,1)S(1)}, u32[]{:S(2)}, u32[]{:S(2)}) %collective-permute-start.11) | collective-permute-done | bytes 262176 | tf_op jit(solution)/shard_map/ppermute | solution.py:77
  144.8 2.4 %first.1 = (bf16[1024,384]{1,0:T(8,128)(2,1)S(1)}, bf16[2048,1024]{1,0:T(8,128)(2,1)S(1)}) custom-call(bf16[2048,384]{1,0:T(8,128)(2,1)S(1)} %assemble.1.rows_ref, bf16[256,1024]{1,0:T(8,128)(2,1)S(1)} %bitcast.11, bf16[256,1024]{1,0:T(8,128)(2,1)S(1)} %collective-permute-done.5.rest_1_, bf16[256,1024]{1,0:T(8,128)(2,1)S(1)} %collective-permute-done.6.rest_2_, ...), custom_call_target="tpu_custom_call" | custom-call | tf_op jit(solution)/shard_map/first/pallas_call | solution.py:202
  147.2 4.2 %second.1 = bf16[1024,768]{1,0:T(8,128)(2,1)} custom-call(s32[3]{0:T(128)S(1)} %pad_add_fusion.refs_0_.where_ref, bf16[2048,384]{1,0:T(8,128)(2,1)S(1)} %collective-permute-done.4.rows_ref, bf16[2048,1024]{1,0:T(8,128)(2,1)S(1)} %get-tuple-element.15.hidden_ref, bf16[1024,384]{1,0:T(8,128)(2,1)S(1)} %get-tuple-element.16.done_ref), custom_call_target="tpu_custom_call" | custom-call | tf_op jit(solution)/shard_map/second/pallas_call | solution.py:213
  (16 shorter events, 2.4 us)
Async XLA Ops:
  0.0 76.5 %copy-start = (bf16[1,256,1024]{2,1,0:T(8,128)(2,1)S(1)}, bf16[1,256,1024]{2,1,0:T(8,128)(2,1)}, u32[]{:S(2)}) copy-start(bf16[1,256,1024]{2,1,0:T(8,128)(2,1)} %param.7) | copy-start | bytes 1572868
  64.0 18.4 %collective-permute-start.2 = (bf16[4,2,32,384]{3,2,1,0:T(8,128)(2,1)S(1)}, bf16[4,2,32,384]{3,2,1,0:T(8,128)(2,1)S(1)}, u32[]{:S(2)}, u32[]{:S(2)}) collective-permute-start(bf16[4,2,32,384]{3,2,1,0:T(8,128)(2,1)S(1)} %get-tuple-element.11), channel_id=1, source_target_pairs={{0,4},{1,5},{2,6},{3,7},{4,8},{5,9},{6,10},{7,11},{8,12},{9,13},{1... | collective-permute-start | bytes 589832 | tf_op jit(solution)/shard_map/ppermute | solution.py:184
  69.4 24.0 %collective-permute-start.1 = (bf16[8,2,32,384]{3,2,1,0:T(8,128)(2,1)S(1)}, bf16[8,2,32,384]{3,2,1,0:T(8,128)(2,1)S(1)}, u32[]{:S(2)}, u32[]{:S(2)}) collective-permute-start(bf16[8,2,32,384]{3,2,1,0:T(8,128)(2,1)S(1)} %all_to_all.17.in_ref.refs_1_), channel_id=1, source_target_pairs={{0,14},{1,15},{2,0},{3,1},{4,2},{5,3},{6,4},{7,5},{8,6},{9,7},{10,... | collective-permute-start | bytes 1179656 | tf_op jit(solution)/shard_map/ppermute | solution.py:183
  72.8 20.6 %collective-permute-start = (bf16[8,2,32,384]{3,2,1,0:T(8,128)(2,1)S(1)}, bf16[8,2,32,384]{3,2,1,0:T(8,128)(2,1)S(1)}, u32[]{:S(2)}, u32[]{:S(2)}) collective-permute-start(bf16[8,2,32,384]{3,2,1,0:T(8,128)(2,1)S(1)} %all_to_all.17.in_ref.refs_1_), channel_id=1, source_target_pairs={{0,2},{1,3},{2,4},{3,5},{4,6},{5,7},{6,8},{7,9},{8,10},{9,11},{10,... | collective-permute-start | bytes 1179656 | tf_op jit(solution)/shard_map/ppermute | solution.py:182
  76.5 19.6 %collective-permute-start.6 = (bf16[256,1024]{1,0:T(8,128)(2,1)S(1)}, bf16[256,1024]{1,0:T(8,128)(2,1)S(1)}, u32[]{:S(2)}, u32[]{:S(2)}) collective-permute-start(bf16[256,1024]{1,0:T(8,128)(2,1)S(1)} %bitcast.9), channel_id=1, source_target_pairs={{0,896},{128,0},{256,128},{384,256},{512,384},{640,512},{768,640},... | collective-permute-start | bytes 1572872 | tf_op jit(solution)/shard_map/ppermute | solution.py:78
  78.4 21.1 %collective-permute-start.5 = (bf16[256,1024]{1,0:T(8,128)(2,1)S(1)}, bf16[256,1024]{1,0:T(8,128)(2,1)S(1)}, u32[]{:S(2)}, u32[]{:S(2)}) collective-permute-start(bf16[256,1024]{1,0:T(8,128)(2,1)S(1)} %bitcast.10), channel_id=1, source_target_pairs={{0,128},{128,256},{256,384},{384,512},{512,640},{640,768},{768,896... | collective-permute-start | bytes 1572872 | tf_op jit(solution)/shard_map/ppermute | solution.py:77
  82.3 11.1 %collective-permute-start.3 = (bf16[4,2,32,384]{3,2,1,0:T(8,128)(2,1)S(1)}, bf16[4,2,32,384]{3,2,1,0:T(8,128)(2,1)S(1)}, u32[]{:S(2)}, u32[]{:S(2)}) collective-permute-start(bf16[4,2,32,384]{3,2,1,0:T(8,128)(2,1)S(1)} %get-tuple-element.12), channel_id=1, source_target_pairs={{0,12},{1,13},{2,14},{3,15},{4,0},{5,1},{6,2},{7,3},{8,4},{9,5},{1... | collective-permute-start | bytes 589832 | tf_op jit(solution)/shard_map/ppermute | solution.py:185
  94.1 53.1 %collective-permute-start.4 = (bf16[2048,384]{1,0:T(8,128)(2,1)S(1)}, bf16[2048,384]{1,0:T(8,128)(2,1)S(1)}, u32[]{:S(2)}, u32[]{:S(2)}) collective-permute-start(bf16[2048,384]{1,0:T(8,128)(2,1)S(1)} %assemble.1.rows_ref), channel_id=1, source_target_pairs={{0,1},{1,0},{2,3},{3,2},{4,5},{5,4},{6,7},{7,6},{8,9},{9,8},{10,11... | collective-permute-start | bytes 4718600 | tf_op jit(solution)/shard_map/ppermute | solution.py:198
  96.1 16.2 %collective-permute-start.8 = (bf16[256,1024]{1,0:T(8,128)(2,1)S(1)}, bf16[256,1024]{1,0:T(8,128)(2,1)S(1)}, u32[]{:S(2)}, u32[]{:S(2)}) collective-permute-start(bf16[256,1024]{1,0:T(8,128)(2,1)S(1)} %collective-permute-done.6.rest_2_), channel_id=1, source_target_pairs={{0,896},{128,0},{256,128},{384,256},{512,384},{640,512},{768,640},... | collective-permute-start | bytes 1572872 | tf_op jit(solution)/shard_map/ppermute | solution.py:78
  99.5 17.4 %collective-permute-start.7 = (bf16[256,1024]{1,0:T(8,128)(2,1)S(1)}, bf16[256,1024]{1,0:T(8,128)(2,1)S(1)}, u32[]{:S(2)}, u32[]{:S(2)}) collective-permute-start(bf16[256,1024]{1,0:T(8,128)(2,1)S(1)} %collective-permute-done.5.rest_1_), channel_id=1, source_target_pairs={{0,128},{128,256},{256,384},{384,512},{512,640},{640,768},{768,896... | collective-permute-start | bytes 1572872 | tf_op jit(solution)/shard_map/ppermute | solution.py:77
  112.3 15.6 %collective-permute-start.10 = (bf16[256,1024]{1,0:T(8,128)(2,1)S(1)}, bf16[256,1024]{1,0:T(8,128)(2,1)S(1)}, u32[]{:S(2)}, u32[]{:S(2)}) collective-permute-start(bf16[256,1024]{1,0:T(8,128)(2,1)S(1)} %collective-permute-done.8.rest_4_), channel_id=1, source_target_pairs={{0,896},{128,0},{256,128},{384,256},{512,384},{640,512},{768,640},... | collective-permute-start | bytes 1572872 | tf_op jit(solution)/shard_map/ppermute | solution.py:78
  116.9 17.3 %collective-permute-start.9 = (bf16[256,1024]{1,0:T(8,128)(2,1)S(1)}, bf16[256,1024]{1,0:T(8,128)(2,1)S(1)}, u32[]{:S(2)}, u32[]{:S(2)}) collective-permute-start(bf16[256,1024]{1,0:T(8,128)(2,1)S(1)} %collective-permute-done.7.rest_3_), channel_id=1, source_target_pairs={{0,128},{128,256},{256,384},{384,512},{512,640},{640,768},{768,896... | collective-permute-start | bytes 1572872 | tf_op jit(solution)/shard_map/ppermute | solution.py:77
  128.6 10.1 %collective-permute-start.12 = (bf16[128,1024]{1,0:T(8,128)(2,1)S(1)}, bf16[128,1024]{1,0:T(8,128)(2,1)S(1)}, u32[]{:S(2)}, u32[]{:S(2)}) collective-permute-start(bf16[128,1024]{1,0:T(8,128)(2,1)S(1)} %get-tuple-element.14), channel_id=1, source_target_pairs={{0,896},{128,0},{256,128},{384,256},{512,384},{640,512},{768,640},... | collective-permute-start | bytes 786440 | tf_op jit(solution)/shard_map/ppermute | solution.py:78
  135.0 9.8 %collective-permute-start.11 = (bf16[128,1024]{1,0:T(8,128)(2,1)S(1)}, bf16[128,1024]{1,0:T(8,128)(2,1)S(1)}, u32[]{:S(2)}, u32[]{:S(2)}) collective-permute-start(bf16[128,1024]{1,0:T(8,128)(2,1)S(1)} %get-tuple-element.13), channel_id=1, source_target_pairs={{0,128},{128,256},{256,384},{384,512},{512,640},{640,768},{768,896... | collective-permute-start | bytes 786440 | tf_op jit(solution)/shard_map/ppermute | solution.py:77

commit v2 on v1

--- a/solution.py
+++ b/solution.py
@@ -42,24 +42,26 @@
         out_ref[e] = (picked * weight).astype(out_ref.dtype)
 
 
-def parts_body(in_ref, *out_refs):
-    at = 0
-    for ref in out_refs:
-        ref[...] = in_ref[at : at + ref.shape[0]]
-        at += ref.shape[0]
-
-
-def two_halves(array):
+def pick_body(where_ref, even_ref, odd_ref, out_ref):
+    @pl.when(where_ref[2] == 0)
+    def _():
+        out_ref[...] = even_ref[...]
+
+    @pl.when(where_ref[2] != 0)
+    def _():
+        out_ref[...] = odd_ref[...]
+
+
+def pick(place, even, odd):
     vmem = pl.BlockSpec(memory_space=pltpu.VMEM)
-    half = pltpu.VMEM((array.shape[0] // 2, *array.shape[1:]), array.dtype)
     return pl.pallas_call(
-        parts_body,
-        out_shape=(half, half),
-        in_specs=[vmem],
-        out_specs=(vmem, vmem),
+        pick_body,
+        out_shape=pltpu.VMEM(even.shape, even.dtype),
+        in_specs=[pl.BlockSpec(memory_space=pltpu.SMEM), vmem, vmem],
+        out_specs=vmem,
         compiler_params=pltpu.CompilerParams(vmem_limit_bytes=2 << 20),
-        name="halves",
-    )(in_vmem(array))
+        name="pick",
+    )(place, in_vmem(even), in_vmem(odd))
 
 
 def twice_body(in_ref, out_ref):
@@ -67,42 +69,41 @@
         out_ref[k] = in_ref[...]
 
 
-def hidden_ring(hidden, up, down, count):
-    half = count // 2
-    below, above = hidden, hidden
-    sources = []
-    for step in range(1, half + 1):
-        if step == half:
-            below, above = two_halves(below)[0], two_halves(above)[1]
+def hidden_ring(hidden, place, count, tensor_count):
+    up = [(k, (k + 1) % count) for k in range(count)]
+    down = [(k, (k - 1) % count) for k in range(count)]
+    below, above, pieces = hidden, hidden, [hidden]
+    for _ in range(1, count // 2):
         below = lax.ppermute(below, "dp", up)
         above = lax.ppermute(above, "dp", down)
-        if step < half:
-            sources += [(-step, [below]), (step, [above])]
-        else:
-            sources.append((half, [below, above]))
-    return sources
+        pieces += [below, above]
+    across = [
+        (y * tensor_count + t, (y + 1 - 2 * (t % CORES)) % count * tensor_count + t)
+        for y in range(count)
+        for t in range(tensor_count)
+    ]
+    last = pick(place, below, above)
+    last = lax.ppermute(last, ("dp", "tensor"), across)
+    return pieces + [last]
 
 
 def assemble_body(count, where_ref, *refs):
     me, mine = where_ref[0], where_ref[1]
-    own_ref, below_ref, above_ref, *far_refs, out_ref = refs
+    own_ref, below_ref, above_ref, far_ref, out_ref = refs
     groups = count // 2
     size = own_ref.shape[1] * own_ref.shape[2]
-    for step, pieces in ((0, [own_ref]), (-1, [below_ref]), (1, [above_ref]), (2, far_refs)):
+    for step, ref in ((0, own_ref), (-1, below_ref), (1, above_ref), (2, far_ref)):
         row = ((mine + step) % groups) * size
-        i = 0
-        for ref in pieces:
-            for k in range(ref.shape[0]):
-                ahead = (i - me) % count
-                place = jnp.where(
-                    ahead <= count // 2,
-                    2 * ahead - jnp.where(ahead == count // 2, 1, 0),
-                    2 * (count - ahead) - 1,
-                )
-                for part in range(ref.shape[1]):
-                    start = place * (groups * size) + row + part * CAP
-                    out_ref[pl.ds(pl.multiple_of(start, CAP), CAP), :] = ref[k, part]
-                i += 1
+        for i in range(count):
+            ahead = (i - me) % count
+            place = jnp.where(
+                ahead <= count // 2,
+                2 * ahead - jnp.where(ahead == count // 2, 1, 0),
+                2 * (count - ahead) - 1,
+            )
+            for part in range(ref.shape[1]):
+                start = place * (groups * size) + row + part * CAP
+                out_ref[pl.ds(pl.multiple_of(start, CAP), CAP), :] = ref[i, part]
 
 
 def products(hidden_ref, rows_ref):
@@ -147,18 +148,19 @@
     width = grad_out.shape[1]
     hidden = saved_hidden[0]
     rows, units = hidden.shape
-    y_up = [(k, (k + 1) % data_count) for k in range(data_count)]
-    y_down = [(k, (k - 1) % data_count) for k in range(data_count)]
-
-    def shift(by):
-        return [(k, (k + by) % tensor_count) for k in range(tensor_count)]
+    groups = chips // 2
+
+    def shift(*by):
+        return [(k, (k + by[k % len(by)]) % tensor_count) for k in range(tensor_count)]
 
     swap = [(k, k ^ 1) for k in range(tensor_count)]
     same_core = [[c + CORES * k for k in range(chips)] for c in range(CORES)]
     smem = pl.BlockSpec(memory_space=pltpu.SMEM)
     vmem = pl.BlockSpec(memory_space=pltpu.VMEM)
 
-    sources = [(0, [hidden])] + hidden_ring(hidden, y_up, y_down, data_count)
+    t = lax.axis_index("tensor")
+    place = jnp.stack([lax.axis_index("dp"), t // CORES % groups, t % CORES]).astype(jnp.int32)
+    pieces = hidden_ring(hidden, place, data_count, tensor_count)
 
     slots = pl.pallas_call(
         lambda *refs: select_body(expert_count, *refs),
@@ -166,7 +168,6 @@
         name="select",
     )(expert_ids.T, route_gates.T, grad_out)
     slots = lax.all_to_all(slots, "expert", 0, 0, tiled=True)
-    groups = chips // 2
     slots = pl.pallas_call(
         twice_body,
         out_shape=jax.ShapeDtypeStruct((2, *slots.shape), slots.dtype),
@@ -178,26 +179,21 @@
     slots = slots.reshape(chips, expert_count // groups, CAP, width)
     slots = lax.all_to_all(slots, "tensor", 0, 0, tiled=True, axis_index_groups=same_core)
     slots = lax.all_to_all(slots, "dp", 0, 0, tiled=True)
-    lower, upper = two_halves(slots)
     below = lax.ppermute(slots, "tensor", shift(CORES))
     above = lax.ppermute(slots, "tensor", shift(-CORES))
-    lower = lax.ppermute(lower, "tensor", shift(2 * CORES))
-    upper = lax.ppermute(upper, "tensor", shift(-2 * CORES))
-
-    t = lax.axis_index("tensor")
-    place = jnp.stack([lax.axis_index("dp"), t // CORES % groups, t % CORES]).astype(jnp.int32)
+    far = lax.ppermute(slots, "tensor", shift(2 * CORES, -2 * CORES))
+
     taken = data_count * rows
     mine = pl.pallas_call(
         lambda *refs: assemble_body(data_count, *refs),
         out_shape=pltpu.VMEM((taken, width), jnp.bfloat16),
-        in_specs=[smem] + [vmem] * 5,
+        in_specs=[smem] + [vmem] * 4,
         out_specs=vmem,
         compiler_params=pltpu.CompilerParams(vmem_limit_bytes=4 << 20),
         name="assemble",
-    )(place, *[in_vmem(p) for p in (slots, below, above, lower, upper)])
+    )(place, *[in_vmem(p) for p in (slots, below, above, far)])
     other = lax.ppermute(mine, "tensor", swap)
 
-    pieces = [p for _, ps in sources for p in ps]
     params = pltpu.CompilerParams(vmem_limit_bytes=14 << 20)
     done, gathered = pl.pallas_call(
         first_body,

time: 152 us -> 132 us (0.87)
  the two profiles are of different devices: /device:TPU:14 before, /device:TPU:1 now
where the time goes in v2:
time: 132 us; the launch traced here: 131 us
  starting transfers between devices  45.6 us (35%)
  blocking collectives  43.9 us (33%)
  waiting for transfers between devices  32.2 us (24%)
  Pallas kernels  9.34 us (7%)
    all_to_all x1, blocking collectives, local(): slots = lax.all_to_all(slots, 'expert', 0, 0, tiled=True)  26 us
    all_to_all x1, blocking collectives, local(): lax.all_to_all(slots, 'tensor', 0, 0, tiled=True, axis_index_groups=same_...  17.9 us
    ppermute x3, starting transfers between devices, hidden_ring(): above = lax.ppermute(above, 'dp', down)  10.7 us
    ppermute x3, waiting for transfers between devices, hidden_ring(): above = lax.ppermute(above, 'dp', down)  10.1 us
    ppermute x1, starting transfers between devices, local(): other = lax.ppermute(mine, 'tensor', swap)  8.64 us
    ppermute x1, waiting for transfers between devices, hidden_ring(): last = lax.ppermute(last, ('dp', 'tensor'), across)  8.08 us
    all_to_all x1, starting transfers between devices, local(): slots = lax.all_to_all(slots, 'dp', 0, 0, tiled=True)  7.28 us
    ppermute x3, starting transfers between devices, hidden_ring(): below = lax.ppermute(below, 'dp', up)  7.2 us
  transfers between devices with their start and end apart: 12, of which 6 were waited for; matrix products, arithmetic and copies ran while one was open for 0% of the time, Pallas kernels for 3%

profile of v2, /device:TPU:1, one launch (start us, length us, event | category | flops | bytes accessed | tf_op | source)
XLA Modules:
  0.0 131.3 jit_solution(8431093099706340355)
XLA Ops:
  0.0 1.4 %select.9 = bf16[8,32,384]{2,1,0:T(8,128)(2,1)S(1)} custom-call(s32[2,128]{1,0:T(2,128)} %bitcast.12, f32[2,128]{1,0:T(2,128)} %bitcast.13, bf16[128,384]{1,0:T(8,128)(2,1)} %refs_2_.1), custom_call_target="tpu_custom_call" | custom-call | tf_op jit(solution)/shard_map/select/pallas_call | solution.py:165
  1.4 26.0 %all_to_all.15.in_ref = bf16[8,32,384]{2,1,0:T(8,128)(2,1)S(1)} all-to-all(bf16[8,32,384]{2,1,0:T(8,128)(2,1)S(1)} %select.9), channel_id=1, replica_groups=mesh['dp'=8,'expert'=8,'tensor'=16] {'expert'}, dimensions={0} | all-to-all | bytes 393216 | tf_op jit(solution)/shard_map/all_to_all | solution.py:170
  27.4 17.9 %all_to_all.16 = bf16[8,2,32,384]{3,2,1,0:T(8,128)(2,1)} all-to-all(bf16[8,2,32,384]{3,2,1,0:T(8,128)(2,1)S(1)} %bitcast.8), channel_id=1, replica_groups={{0,2,4,6,8,10,12,14},{1,3,5,7,9,11,13,15},{16,18,20,22,24,26,28,30},{17..., dimensions={0} | all-to-all | bytes 786432 | tf_op jit(solution)/shard_map/all_to_all | solution.py:180
  45.3 7.3 %all-to-all-start.2 = ((bf16[8,2,32,384]{3,2,1,0:T(8,128)(2,1)}), bf16[8,2,32,384]{3,2,1,0:T(8,128)(2,1)S(1)}, u32[]{:S(2)}, u32[]{:S(2)}) async-start(bf16[8,2,32,384]{3,2,1,0:T(8,128)(2,1)} %all_to_all.16), calls=%async_computation.2 | async-start | bytes 786432 | tf_op jit(solution)/shard_map/all_to_all | solution.py:181
  52.6 4.6 %collective-permute-start.5 = (bf16[256,1024]{1,0:T(8,128)(2,1)S(1)}, bf16[256,1024]{1,0:T(8,128)(2,1)S(1)}, u32[]{:S(2)}, u32[]{:S(2)}) collective-permute-start(bf16[256,1024]{1,0:T(8,128)(2,1)S(1)} %bitcast.9), channel_id=1, source_target_pairs={{0,896},{128,0},{256,128},{384,256},{512,384},{640,512},{768,640},... | collective-permute-start | bytes 1572872 | tf_op jit(solution)/shard_map/ppermute | solution.py:78
  57.2 1.9 %collective-permute-start.4 = (bf16[256,1024]{1,0:T(8,128)(2,1)S(1)}, bf16[256,1024]{1,0:T(8,128)(2,1)S(1)}, u32[]{:S(2)}, u32[]{:S(2)}) collective-permute-start(bf16[256,1024]{1,0:T(8,128)(2,1)S(1)} %bitcast.10), channel_id=1, source_target_pairs={{0,128},{128,256},{256,384},{384,512},{512,640},{640,768},{768,896... | collective-permute-start | bytes 1572872 | tf_op jit(solution)/shard_map/ppermute | solution.py:77
  59.1 4.3 %all-to-all-done.2.refs_1_ = bf16[8,2,32,384]{3,2,1,0:T(8,128)(2,1)S(1)} async-done(((bf16[8,2,32,384]{3,2,1,0:T(8,128)(2,1)}), bf16[8,2,32,384]{3,2,1,0:T(8,128)(2,1)S(1)}, u32[]{:S(2)}, u32[]{:S(2)}) %all-to-all-start.2) | async-done | bytes 393248 | tf_op jit(solution)/shard_map/all_to_all | solution.py:181
  63.4 4.3 %collective-permute-start.2 = (bf16[8,2,32,384]{3,2,1,0:T(8,128)(2,1)S(1)}, bf16[8,2,32,384]{3,2,1,0:T(8,128)(2,1)S(1)}, u32[]{:S(2)}, u32[]{:S(2)}) collective-permute-start(bf16[8,2,32,384]{3,2,1,0:T(8,128)(2,1)S(1)} %all-to-all-done.2.refs_1_), channel_id=1, source_target_pairs={{0,4},{1,13},{2,6},{3,15},{4,8},{5,1},{6,10},{7,3},{8,12},{9,5},{1... | collective-permute-start | bytes 1179656 | tf_op jit(solution)/shard_map/ppermute | solution.py:184
  67.7 1.9 %collective-permute-start.1 = (bf16[8,2,32,384]{3,2,1,0:T(8,128)(2,1)S(1)}, bf16[8,2,32,384]{3,2,1,0:T(8,128)(2,1)S(1)}, u32[]{:S(2)}, u32[]{:S(2)}) collective-permute-start(bf16[8,2,32,384]{3,2,1,0:T(8,128)(2,1)S(1)} %all-to-all-done.2.refs_1_), channel_id=1, source_target_pairs={{0,14},{1,15},{2,0},{3,1},{4,2},{5,3},{6,4},{7,5},{8,6},{9,7},{10,... | collective-permute-start | bytes 1179656 | tf_op jit(solution)/shard_map/ppermute | solution.py:183
  69.6 3.4 %collective-permute-start = (bf16[8,2,32,384]{3,2,1,0:T(8,128)(2,1)S(1)}, bf16[8,2,32,384]{3,2,1,0:T(8,128)(2,1)S(1)}, u32[]{:S(2)}, u32[]{:S(2)}) collective-permute-start(bf16[8,2,32,384]{3,2,1,0:T(8,128)(2,1)S(1)} %all-to-all-done.2.refs_1_), channel_id=1, source_target_pairs={{0,2},{1,3},{2,4},{3,5},{4,6},{5,7},{6,8},{7,9},{8,10},{9,11},{10,... | collective-permute-start | bytes 1179656 | tf_op jit(solution)/shard_map/ppermute | solution.py:182
  73.1 4.2 %collective-permute-start.7 = (bf16[256,1024]{1,0:T(8,128)(2,1)S(1)}, bf16[256,1024]{1,0:T(8,128)(2,1)S(1)}, u32[]{:S(2)}, u32[]{:S(2)}) collective-permute-start(bf16[256,1024]{1,0:T(8,128)(2,1)S(1)} %collective-permute-done.5.rest_2_), channel_id=1, source_target_pairs={{0,896},{128,0},{256,128},{384,256},{512,384},{640,512},{768,640},... | collective-permute-start | bytes 1572872 | tf_op jit(solution)/shard_map/ppermute | solution.py:78
  77.4 1.9 %collective-permute-start.6 = (bf16[256,1024]{1,0:T(8,128)(2,1)S(1)}, bf16[256,1024]{1,0:T(8,128)(2,1)S(1)}, u32[]{:S(2)}, u32[]{:S(2)}) collective-permute-start(bf16[256,1024]{1,0:T(8,128)(2,1)S(1)} %collective-permute-done.4.rest_1_), channel_id=1, source_target_pairs={{0,128},{128,256},{256,384},{384,512},{512,640},{640,768},{768,896... | collective-permute-start | bytes 1572872 | tf_op jit(solution)/shard_map/ppermute | solution.py:77
  79.3 0.9 collective-permute-done.1.refs_3_
  80.2 5.7 %collective-permute-done.refs_2_ = bf16[8,2,32,384]{3,2,1,0:T(8,128)(2,1)S(1)} collective-permute-done((bf16[8,2,32,384]{3,2,1,0:T(8,128)(2,1)S(1)}, bf16[8,2,32,384]{3,2,1,0:T(8,128)(2,1)S(1)}, u32[]{:S(2)}, u32[]{:S(2)}) %collective-permute-start) | collective-permute-done | bytes 393248 | tf_op jit(solution)/shard_map/ppermute | solution.py:182
  85.9 0.7 assemble.1.rows_ref
  86.7 8.6 %collective-permute-start.3 = (bf16[2048,384]{1,0:T(8,128)(2,1)S(1)}, bf16[2048,384]{1,0:T(8,128)(2,1)S(1)}, u32[]{:S(2)}, u32[]{:S(2)}) collective-permute-start(bf16[2048,384]{1,0:T(8,128)(2,1)S(1)} %assemble.1.rows_ref), channel_id=1, source_target_pairs={{0,1},{1,0},{2,3},{3,2},{4,5},{5,4},{6,7},{7,6},{8,9},{9,8},{10,11... | collective-permute-start | bytes 4718600 | tf_op jit(solution)/shard_map/ppermute | solution.py:195
  95.3 1.9 %collective-permute-start.9 = (bf16[256,1024]{1,0:T(8,128)(2,1)S(1)}, bf16[256,1024]{1,0:T(8,128)(2,1)S(1)}, u32[]{:S(2)}, u32[]{:S(2)}) collective-permute-start(bf16[256,1024]{1,0:T(8,128)(2,1)S(1)} %collective-permute-done.7.rest_4_), channel_id=1, source_target_pairs={{0,896},{128,0},{256,128},{384,256},{512,384},{640,512},{768,640},... | collective-permute-start | bytes 1572872 | tf_op jit(solution)/shard_map/ppermute | solution.py:78
  97.3 3.4 %collective-permute-start.8 = (bf16[256,1024]{1,0:T(8,128)(2,1)S(1)}, bf16[256,1024]{1,0:T(8,128)(2,1)S(1)}, u32[]{:S(2)}, u32[]{:S(2)}) collective-permute-start(bf16[256,1024]{1,0:T(8,128)(2,1)S(1)} %collective-permute-done.6.rest_3_), channel_id=1, source_target_pairs={{0,128},{128,256},{256,384},{384,512},{512,640},{640,768},{768,896... | collective-permute-start | bytes 1572872 | tf_op jit(solution)/shard_map/ppermute | solution.py:77
  100.6 10.1 %collective-permute-done.9.odd_ref.rest_6_ = bf16[256,1024]{1,0:T(8,128)(2,1)S(1)} collective-permute-done((bf16[256,1024]{1,0:T(8,128)(2,1)S(1)}, bf16[256,1024]{1,0:T(8,128)(2,1)S(1)}, u32[]{:S(2)}, u32[]{:S(2)}) %collective-permute-start.9) | collective-permute-done | bytes 524320 | tf_op jit(solution)/shard_map/ppermute | solution.py:78
  110.7 3.1 %collective-permute-done.8.even_ref.rest_5_ = bf16[256,1024]{1,0:T(8,128)(2,1)S(1)} collective-permute-done((bf16[256,1024]{1,0:T(8,128)(2,1)S(1)}, bf16[256,1024]{1,0:T(8,128)(2,1)S(1)}, u32[]{:S(2)}, u32[]{:S(2)}) %collective-permute-start.8) | collective-permute-done | bytes 524320 | tf_op jit(solution)/shard_map/ppermute | solution.py:77
  114.4 2.1 %collective-permute-start.10 = (bf16[256,1024]{1,0:T(8,128)(2,1)S(1)}, bf16[256,1024]{1,0:T(8,128)(2,1)S(1)}, u32[]{:S(2)}, u32[]{:S(2)}) collective-permute-start(bf16[256,1024]{1,0:T(8,128)(2,1)S(1)} %pick.1), channel_id=1, source_target_pairs={{0,128},{1,897},{2,130},{3,899},{4,132},{5,901},{6,134},{7,903},{8... | collective-permute-start | bytes 1572872 | tf_op jit(solution)/shard_map/ppermute | solution.py:86
  116.6 8.1 %collective-permute-done.10.rest_7_ = bf16[256,1024]{1,0:T(8,128)(2,1)S(1)} collective-permute-done((bf16[256,1024]{1,0:T(8,128)(2,1)S(1)}, bf16[256,1024]{1,0:T(8,128)(2,1)S(1)}, u32[]{:S(2)}, u32[]{:S(2)}) %collective-permute-start.10) | collective-permute-done | bytes 524320 | tf_op jit(solution)/shard_map/ppermute | solution.py:86
  124.7 2.4 %first.1 = (bf16[1024,384]{1,0:T(8,128)(2,1)S(1)}, bf16[2048,1024]{1,0:T(8,128)(2,1)S(1)}) custom-call(bf16[2048,384]{1,0:T(8,128)(2,1)S(1)} %assemble.1.rows_ref, bf16[256,1024]{1,0:T(8,128)(2,1)S(1)} %bitcast.11, bf16[256,1024]{1,0:T(8,128)(2,1)S(1)} %collective-permute-done.4.rest_1_, bf16[256,1024]{1,0:T(8,128)(2,1)S(1)} %collective-permute-done.5.rest_2_, ...), custom_call_target="tpu_custom_call" | custom-call | tf_op jit(solution)/shard_map/first/pallas_call | solution.py:198
  127.1 4.2 %second.1 = bf16[1024,768]{1,0:T(8,128)(2,1)} custom-call(s32[3]{0:T(128)S(1)} %pad_add_fusion.refs_0_.where_ref, bf16[2048,384]{1,0:T(8,128)(2,1)S(1)} %collective-permute-done.3.rows_ref, bf16[2048,1024]{1,0:T(8,128)(2,1)S(1)} %get-tuple-element.7.hidden_ref, bf16[1024,384]{1,0:T(8,128)(2,1)S(1)} %get-tuple-element.8.done_ref), custom_call_target="tpu_custom_call" | custom-call | tf_op jit(solution)/shard_map/second/pallas_call | solution.py:209
  (11 shorter events, 0.7 us)
Async XLA Ops:
  0.0 52.6 %copy-start = (bf16[1,256,1024]{2,1,0:T(8,128)(2,1)S(1)}, bf16[1,256,1024]{2,1,0:T(8,128)(2,1)}, u32[]{:S(2)}) copy-start(bf16[1,256,1024]{2,1,0:T(8,128)(2,1)} %param.7) | copy-start | bytes 1572868
  45.3 18.0 %all-to-all-start.2 = ((bf16[8,2,32,384]{3,2,1,0:T(8,128)(2,1)}), bf16[8,2,32,384]{3,2,1,0:T(8,128)(2,1)S(1)}, u32[]{:S(2)}, u32[]{:S(2)}) async-start(bf16[8,2,32,384]{3,2,1,0:T(8,128)(2,1)} %all_to_all.16), calls=%async_computation.2 | async-start | bytes 786432 | tf_op jit(solution)/shard_map/all_to_all | solution.py:181
  52.6 20.5 %collective-permute-start.5 = (bf16[256,1024]{1,0:T(8,128)(2,1)S(1)}, bf16[256,1024]{1,0:T(8,128)(2,1)S(1)}, u32[]{:S(2)}, u32[]{:S(2)}) collective-permute-start(bf16[256,1024]{1,0:T(8,128)(2,1)S(1)} %bitcast.9), channel_id=1, source_target_pairs={{0,896},{128,0},{256,128},{384,256},{512,384},{640,512},{768,640},... | collective-permute-start | bytes 1572872 | tf_op jit(solution)/shard_map/ppermute | solution.py:78
  57.2 20.2 %collective-permute-start.4 = (bf16[256,1024]{1,0:T(8,128)(2,1)S(1)}, bf16[256,1024]{1,0:T(8,128)(2,1)S(1)}, u32[]{:S(2)}, u32[]{:S(2)}) collective-permute-start(bf16[256,1024]{1,0:T(8,128)(2,1)S(1)} %bitcast.10), channel_id=1, source_target_pairs={{0,128},{128,256},{256,384},{384,512},{512,640},{640,768},{768,896... | collective-permute-start | bytes 1572872 | tf_op jit(solution)/shard_map/ppermute | solution.py:77
  63.4 15.9 %collective-permute-start.2 = (bf16[8,2,32,384]{3,2,1,0:T(8,128)(2,1)S(1)}, bf16[8,2,32,384]{3,2,1,0:T(8,128)(2,1)S(1)}, u32[]{:S(2)}, u32[]{:S(2)}) collective-permute-start(bf16[8,2,32,384]{3,2,1,0:T(8,128)(2,1)S(1)} %all-to-all-done.2.refs_1_), channel_id=1, source_target_pairs={{0,4},{1,13},{2,6},{3,15},{4,8},{5,1},{6,10},{7,3},{8,12},{9,5},{1... | collective-permute-start | bytes 1179656 | tf_op jit(solution)/shard_map/ppermute | solution.py:184
  67.7 12.5 %collective-permute-start.1 = (bf16[8,2,32,384]{3,2,1,0:T(8,128)(2,1)S(1)}, bf16[8,2,32,384]{3,2,1,0:T(8,128)(2,1)S(1)}, u32[]{:S(2)}, u32[]{:S(2)}) collective-permute-start(bf16[8,2,32,384]{3,2,1,0:T(8,128)(2,1)S(1)} %all-to-all-done.2.refs_1_), channel_id=1, source_target_pairs={{0,14},{1,15},{2,0},{3,1},{4,2},{5,3},{6,4},{7,5},{8,6},{9,7},{10,... | collective-permute-start | bytes 1179656 | tf_op jit(solution)/shard_map/ppermute | solution.py:183
  69.6 16.3 %collective-permute-start = (bf16[8,2,32,384]{3,2,1,0:T(8,128)(2,1)S(1)}, bf16[8,2,32,384]{3,2,1,0:T(8,128)(2,1)S(1)}, u32[]{:S(2)}, u32[]{:S(2)}) collective-permute-start(bf16[8,2,32,384]{3,2,1,0:T(8,128)(2,1)S(1)} %all-to-all-done.2.refs_1_), channel_id=1, source_target_pairs={{0,2},{1,3},{2,4},{3,5},{4,6},{5,7},{6,8},{7,9},{8,10},{9,11},{10,... | collective-permute-start | bytes 1179656 | tf_op jit(solution)/shard_map/ppermute | solution.py:182
  73.1 22.2 %collective-permute-start.7 = (bf16[256,1024]{1,0:T(8,128)(2,1)S(1)}, bf16[256,1024]{1,0:T(8,128)(2,1)S(1)}, u32[]{:S(2)}, u32[]{:S(2)}) collective-permute-start(bf16[256,1024]{1,0:T(8,128)(2,1)S(1)} %collective-permute-done.5.rest_2_), channel_id=1, source_target_pairs={{0,896},{128,0},{256,128},{384,256},{512,384},{640,512},{768,640},... | collective-permute-start | bytes 1572872 | tf_op jit(solution)/shard_map/ppermute | solution.py:78
  77.4 19.9 %collective-permute-start.6 = (bf16[256,1024]{1,0:T(8,128)(2,1)S(1)}, bf16[256,1024]{1,0:T(8,128)(2,1)S(1)}, u32[]{:S(2)}, u32[]{:S(2)}) collective-permute-start(bf16[256,1024]{1,0:T(8,128)(2,1)S(1)} %collective-permute-done.4.rest_1_), channel_id=1, source_target_pairs={{0,128},{128,256},{256,384},{384,512},{512,640},{640,768},{768,896... | collective-permute-start | bytes 1572872 | tf_op jit(solution)/shard_map/ppermute | solution.py:77
  86.7 40.4 %collective-permute-start.3 = (bf16[2048,384]{1,0:T(8,128)(2,1)S(1)}, bf16[2048,384]{1,0:T(8,128)(2,1)S(1)}, u32[]{:S(2)}, u32[]{:S(2)}) collective-permute-start(bf16[2048,384]{1,0:T(8,128)(2,1)S(1)} %assemble.1.rows_ref), channel_id=1, source_target_pairs={{0,1},{1,0},{2,3},{3,2},{4,5},{5,4},{6,7},{7,6},{8,9},{9,8},{10,11... | collective-permute-start | bytes 4718600 | tf_op jit(solution)/shard_map/ppermute | solution.py:195
  95.3 15.4 %collective-permute-start.9 = (bf16[256,1024]{1,0:T(8,128)(2,1)S(1)}, bf16[256,1024]{1,0:T(8,128)(2,1)S(1)}, u32[]{:S(2)}, u32[]{:S(2)}) collective-permute-start(bf16[256,1024]{1,0:T(8,128)(2,1)S(1)} %collective-permute-done.7.rest_4_), channel_id=1, source_target_pairs={{0,896},{128,0},{256,128},{384,256},{512,384},{640,512},{768,640},... | collective-permute-start | bytes 1572872 | tf_op jit(solution)/shard_map/ppermute | solution.py:78
  97.3 16.6 %collective-permute-start.8 = (bf16[256,1024]{1,0:T(8,128)(2,1)S(1)}, bf16[256,1024]{1,0:T(8,128)(2,1)S(1)}, u32[]{:S(2)}, u32[]{:S(2)}) collective-permute-start(bf16[256,1024]{1,0:T(8,128)(2,1)S(1)} %collective-permute-done.6.rest_3_), channel_id=1, source_target_pairs={{0,128},{128,256},{256,384},{384,512},{512,640},{640,768},{768,896... | collective-permute-start | bytes 1572872 | tf_op jit(solution)/shard_map/ppermute | solution.py:77
  114.4 10.2 %collective-permute-start.10 = (bf16[256,1024]{1,0:T(8,128)(2,1)S(1)}, bf16[256,1024]{1,0:T(8,128)(2,1)S(1)}, u32[]{:S(2)}, u32[]{:S(2)}) collective-permute-start(bf16[256,1024]{1,0:T(8,128)(2,1)S(1)} %pick.1), channel_id=1, source_target_pairs={{0,128},{1,897},{2,130},{3,899},{4,132},{5,901},{6,134},{7,903},{8... | collective-permute-start | bytes 1572872 | tf_op jit(solution)/shard_map/ppermute | solution.py:86

commit v3 on v2

--- a/solution.py
+++ b/solution.py
@@ -128,16 +128,30 @@
         out_ref[units, :] = total.astype(out_ref.dtype)
 
 
-def second_body(where_ref, rows_ref, hidden_ref, done_ref, out_ref):
+def second_body(where_ref, rows_ref, hidden_ref, done_ref, out_ref, block_ref, sems):
     width, core = rows_ref.shape[-1], where_ref[2]
-    out_ref[:, pl.ds(pl.multiple_of(core * width, 128), width)] = done_ref[...]
-    column = pl.multiple_of((1 - core) * width, 128)
+    own = pl.ds(pl.multiple_of(core * width, 128), width)
+    rest = pl.ds(pl.multiple_of((1 - core) * width, 128), width)
+    copies = [pltpu.make_async_copy(done_ref, out_ref.at[:, own], sems.at[0])]
+    copies[0].start()
     for units, total in products(hidden_ref, rows_ref):
-        out_ref[units, pl.ds(column, width)] = total.astype(out_ref.dtype)
+        block_ref[units, :] = total.astype(block_ref.dtype)
+        copies.append(
+            pltpu.make_async_copy(
+                block_ref.at[units], out_ref.at[units, rest], sems.at[len(copies)]
+            )
+        )
+        copies[-1].start()
+    for copy in copies:
+        copy.wait()
 
 
 def in_vmem(array):
     return pltpu.with_memory_space_constraint(array, pltpu.VMEM)
+
+
+def in_hbm(array):
+    return pltpu.with_memory_space_constraint(array, pltpu.HBM)
 
 
 def local(grad_out, expert_ids, route_gates, saved_hidden):
@@ -205,12 +219,13 @@
         out_specs=(vmem, vmem),
         compiler_params=params,
         name="first",
-    )(in_vmem(mine), *pieces)
+    )(in_vmem(mine), *[in_hbm(p) if n in (1, 2, 3) else p for n, p in enumerate(pieces)])
     out = pl.pallas_call(
         second_body,
         out_shape=jax.ShapeDtypeStruct((units, CORES * width), jnp.bfloat16),
         in_specs=[smem] + [vmem] * 3,
-        out_specs=vmem,
+        out_specs=pl.BlockSpec(memory_space=pl.ANY),
+        scratch_shapes=[pltpu.VMEM((units, width), jnp.bfloat16), pltpu.SemaphoreType.DMA((5,))],
         compiler_params=params,
         name="second",
     )(place, in_vmem(other), in_vmem(gathered), in_vmem(done))

time: 132 us -> 133 us (level)
    pallas_call x1, Pallas kernels: 2.42 us -> 3.77 us  [local(): pl.pallas_call(first_body, out_shape=(pltpu.VMEM((units, width), jnp.bflo...]
  transfers between devices with their start and end apart: 12 -> 12, of which waited for: 6 -> 6; matrix products, arithmetic and copies ran while one was open for 0% -> 0% of each run, Pallas kernels for 3% -> 4%
where the time goes in v3:
time: 133 us; the launch traced here: 132 us
  starting transfers between devices  45.6 us (34%)
  blocking collectives  43.9 us (33%)
  waiting for transfers between devices  32.2 us (24%)
  Pallas kernels  10.2 us (8%)
    all_to_all x1, blocking collectives, local(): slots = lax.all_to_all(slots, 'expert', 0, 0, tiled=True)  26 us
    all_to_all x1, blocking collectives, local(): lax.all_to_all(slots, 'tensor', 0, 0, tiled=True, axis_index_groups=same_...  17.9 us
    ppermute x3, starting transfers between devices, hidden_ring(): above = lax.ppermute(above, 'dp', down)  10.7 us
    ppermute x3, waiting for transfers between devices, hidden_ring(): above = lax.ppermute(above, 'dp', down)  10 us
    ppermute x1, starting transfers between devices, local(): other = lax.ppermute(mine, 'tensor', swap)  8.64 us
    ppermute x1, waiting for transfers between devices, hidden_ring(): last = lax.ppermute(last, ('dp', 'tensor'), across)  8.08 us
    all_to_all x1, starting transfers between devices, local(): slots = lax.all_to_all(slots, 'dp', 0, 0, tiled=True)  7.28 us
    ppermute x3, starting transfers between devices, hidden_ring(): below = lax.ppermute(below, 'dp', up)  7.2 us
  transfers between devices with their start and end apart: 12, of which 6 were waited for; matrix products, arithmetic and copies ran while one was open for 0% of the time, Pallas kernels for 4%

profile of v3, /device:TPU:1, one launch (start us, length us, event | category | flops | bytes accessed | tf_op | source)
XLA Modules:
  0.0 132.2 jit_solution(26943304027929390)
XLA Ops:
  0.0 1.4 %select.9 = bf16[8,32,384]{2,1,0:T(8,128)(2,1)S(1)} custom-call(s32[2,128]{1,0:T(2,128)} %bitcast.12, f32[2,128]{1,0:T(2,128)} %bitcast.13, bf16[128,384]{1,0:T(8,128)(2,1)} %refs_2_.1), custom_call_target="tpu_custom_call" | custom-call | tf_op jit(solution)/shard_map/select/pallas_call | solution.py:179
  1.4 26.0 %all_to_all.15.in_ref = bf16[8,32,384]{2,1,0:T(8,128)(2,1)S(1)} all-to-all(bf16[8,32,384]{2,1,0:T(8,128)(2,1)S(1)} %select.9), channel_id=1, replica_groups=mesh['dp'=8,'expert'=8,'tensor'=16] {'expert'}, dimensions={0} | all-to-all | bytes 393216 | tf_op jit(solution)/shard_map/all_to_all | solution.py:184
  27.4 17.9 %all_to_all.16 = bf16[8,2,32,384]{3,2,1,0:T(8,128)(2,1)} all-to-all(bf16[8,2,32,384]{3,2,1,0:T(8,128)(2,1)S(1)} %bitcast.8), channel_id=1, replica_groups={{0,2,4,6,8,10,12,14},{1,3,5,7,9,11,13,15},{16,18,20,22,24,26,28,30},{17..., dimensions={0} | all-to-all | bytes 786432 | tf_op jit(solution)/shard_map/all_to_all | solution.py:194
  45.3 7.3 %all-to-all-start.2 = ((bf16[8,2,32,384]{3,2,1,0:T(8,128)(2,1)}), bf16[8,2,32,384]{3,2,1,0:T(8,128)(2,1)S(1)}, u32[]{:S(2)}, u32[]{:S(2)}) async-start(bf16[8,2,32,384]{3,2,1,0:T(8,128)(2,1)} %all_to_all.16), calls=%async_computation.2 | async-start | bytes 786432 | tf_op jit(solution)/shard_map/all_to_all | solution.py:195
  52.6 4.6 %collective-permute-start.5 = (bf16[256,1024]{1,0:T(8,128)(2,1)S(1)}, bf16[256,1024]{1,0:T(8,128)(2,1)S(1)}, u32[]{:S(2)}, u32[]{:S(2)}) collective-permute-start(bf16[256,1024]{1,0:T(8,128)(2,1)S(1)} %bitcast.9), channel_id=1, source_target_pairs={{0,896},{128,0},{256,128},{384,256},{512,384},{640,512},{768,640},... | collective-permute-start | bytes 1572872 | tf_op jit(solution)/shard_map/ppermute | solution.py:78
  57.2 1.9 %collective-permute-start.4 = (bf16[256,1024]{1,0:T(8,128)(2,1)S(1)}, bf16[256,1024]{1,0:T(8,128)(2,1)S(1)}, u32[]{:S(2)}, u32[]{:S(2)}) collective-permute-start(bf16[256,1024]{1,0:T(8,128)(2,1)S(1)} %bitcast.10), channel_id=1, source_target_pairs={{0,128},{128,256},{256,384},{384,512},{512,640},{640,768},{768,896... | collective-permute-start | bytes 1572872 | tf_op jit(solution)/shard_map/ppermute | solution.py:77
  59.1 4.3 %all-to-all-done.2.refs_1_ = bf16[8,2,32,384]{3,2,1,0:T(8,128)(2,1)S(1)} async-done(((bf16[8,2,32,384]{3,2,1,0:T(8,128)(2,1)}), bf16[8,2,32,384]{3,2,1,0:T(8,128)(2,1)S(1)}, u32[]{:S(2)}, u32[]{:S(2)}) %all-to-all-start.2) | async-done | bytes 393248 | tf_op jit(solution)/shard_map/all_to_all | solution.py:195
  63.4 4.3 %collective-permute-start.2 = (bf16[8,2,32,384]{3,2,1,0:T(8,128)(2,1)S(1)}, bf16[8,2,32,384]{3,2,1,0:T(8,128)(2,1)S(1)}, u32[]{:S(2)}, u32[]{:S(2)}) collective-permute-start(bf16[8,2,32,384]{3,2,1,0:T(8,128)(2,1)S(1)} %all-to-all-done.2.refs_1_), channel_id=1, source_target_pairs={{0,4},{1,13},{2,6},{3,15},{4,8},{5,1},{6,10},{7,3},{8,12},{9,5},{1... | collective-permute-start | bytes 1179656 | tf_op jit(solution)/shard_map/ppermute | solution.py:198
  67.7 1.9 %collective-permute-start.1 = (bf16[8,2,32,384]{3,2,1,0:T(8,128)(2,1)S(1)}, bf16[8,2,32,384]{3,2,1,0:T(8,128)(2,1)S(1)}, u32[]{:S(2)}, u32[]{:S(2)}) collective-permute-start(bf16[8,2,32,384]{3,2,1,0:T(8,128)(2,1)S(1)} %all-to-all-done.2.refs_1_), channel_id=1, source_target_pairs={{0,14},{1,15},{2,0},{3,1},{4,2},{5,3},{6,4},{7,5},{8,6},{9,7},{10,... | collective-permute-start | bytes 1179656 | tf_op jit(solution)/shard_map/ppermute | solution.py:197
  69.6 3.4 %collective-permute-start = (bf16[8,2,32,384]{3,2,1,0:T(8,128)(2,1)S(1)}, bf16[8,2,32,384]{3,2,1,0:T(8,128)(2,1)S(1)}, u32[]{:S(2)}, u32[]{:S(2)}) collective-permute-start(bf16[8,2,32,384]{3,2,1,0:T(8,128)(2,1)S(1)} %all-to-all-done.2.refs_1_), channel_id=1, source_target_pairs={{0,2},{1,3},{2,4},{3,5},{4,6},{5,7},{6,8},{7,9},{8,10},{9,11},{10,... | collective-permute-start | bytes 1179656 | tf_op jit(solution)/shard_map/ppermute | solution.py:196
  73.1 4.2 %collective-permute-start.7 = (bf16[256,1024]{1,0:T(8,128)(2,1)S(1)}, bf16[256,1024]{1,0:T(8,128)(2,1)S(1)}, u32[]{:S(2)}, u32[]{:S(2)}) collective-permute-start(bf16[256,1024]{1,0:T(8,128)(2,1)S(1)} %collective-permute-done.5.rest_2_), channel_id=1, source_target_pairs={{0,896},{128,0},{256,128},{384,256},{512,384},{640,512},{768,640},... | collective-permute-start | bytes 1572872 | tf_op jit(solution)/shard_map/ppermute | solution.py:78
  77.4 1.9 %collective-permute-start.6 = (bf16[256,1024]{1,0:T(8,128)(2,1)S(1)}, bf16[256,1024]{1,0:T(8,128)(2,1)S(1)}, u32[]{:S(2)}, u32[]{:S(2)}) collective-permute-start(bf16[256,1024]{1,0:T(8,128)(2,1)S(1)} %collective-permute-done.4.rest_1_), channel_id=1, source_target_pairs={{0,128},{128,256},{256,384},{384,512},{512,640},{640,768},{768,896... | collective-permute-start | bytes 1572872 | tf_op jit(solution)/shard_map/ppermute | solution.py:77
  79.3 0.9 collective-permute-done.1.refs_3_
  80.2 5.7 %collective-permute-done.refs_2_ = bf16[8,2,32,384]{3,2,1,0:T(8,128)(2,1)S(1)} collective-permute-done((bf16[8,2,32,384]{3,2,1,0:T(8,128)(2,1)S(1)}, bf16[8,2,32,384]{3,2,1,0:T(8,128)(2,1)S(1)}, u32[]{:S(2)}, u32[]{:S(2)}) %collective-permute-start) | collective-permute-done | bytes 393248 | tf_op jit(solution)/shard_map/ppermute | solution.py:196
  85.9 0.7 assemble.1.rows_ref
  86.7 8.6 %collective-permute-start.3 = (bf16[2048,384]{1,0:T(8,128)(2,1)S(1)}, bf16[2048,384]{1,0:T(8,128)(2,1)S(1)}, u32[]{:S(2)}, u32[]{:S(2)}) collective-permute-start(bf16[2048,384]{1,0:T(8,128)(2,1)S(1)} %assemble.1.rows_ref), channel_id=1, source_target_pairs={{0,1},{1,0},{2,3},{3,2},{4,5},{5,4},{6,7},{7,6},{8,9},{9,8},{10,11... | collective-permute-start | bytes 4718600 | tf_op jit(solution)/shard_map/ppermute | solution.py:209
  95.4 1.9 %collective-permute-start.9 = (bf16[256,1024]{1,0:T(8,128)(2,1)S(1)}, bf16[256,1024]{1,0:T(8,128)(2,1)S(1)}, u32[]{:S(2)}, u32[]{:S(2)}) collective-permute-start(bf16[256,1024]{1,0:T(8,128)(2,1)S(1)} %collective-permute-done.7.rest_4_), channel_id=1, source_target_pairs={{0,896},{128,0},{256,128},{384,256},{512,384},{640,512},{768,640},... | collective-permute-start | bytes 1572872 | tf_op jit(solution)/shard_map/ppermute | solution.py:78
  97.3 3.4 %collective-permute-start.8 = (bf16[256,1024]{1,0:T(8,128)(2,1)S(1)}, bf16[256,1024]{1,0:T(8,128)(2,1)S(1)}, u32[]{:S(2)}, u32[]{:S(2)}) collective-permute-start(bf16[256,1024]{1,0:T(8,128)(2,1)S(1)} %collective-permute-done.6.rest_3_), channel_id=1, source_target_pairs={{0,128},{128,256},{256,384},{384,512},{512,640},{640,768},{768,896... | collective-permute-start | bytes 1572872 | tf_op jit(solution)/shard_map/ppermute | solution.py:77
  100.7 10.0 %collective-permute-done.9.odd_ref.rest_6_ = bf16[256,1024]{1,0:T(8,128)(2,1)S(1)} collective-permute-done((bf16[256,1024]{1,0:T(8,128)(2,1)S(1)}, bf16[256,1024]{1,0:T(8,128)(2,1)S(1)}, u32[]{:S(2)}, u32[]{:S(2)}) %collective-permute-start.9) | collective-permute-done | bytes 524320 | tf_op jit(solution)/shard_map/ppermute | solution.py:78
  110.7 3.2 %collective-permute-done.8.even_ref.rest_5_ = bf16[256,1024]{1,0:T(8,128)(2,1)S(1)} collective-permute-done((bf16[256,1024]{1,0:T(8,128)(2,1)S(1)}, bf16[256,1024]{1,0:T(8,128)(2,1)S(1)}, u32[]{:S(2)}, u32[]{:S(2)}) %collective-permute-start.8) | collective-permute-done | bytes 524320 | tf_op jit(solution)/shard_map/ppermute | solution.py:77
  114.5 2.1 %collective-permute-start.10 = (bf16[256,1024]{1,0:T(8,128)(2,1)S(1)}, bf16[256,1024]{1,0:T(8,128)(2,1)S(1)}, u32[]{:S(2)}, u32[]{:S(2)}) collective-permute-start(bf16[256,1024]{1,0:T(8,128)(2,1)S(1)} %pick.1), channel_id=1, source_target_pairs={{0,128},{1,897},{2,130},{3,899},{4,132},{5,901},{6,134},{7,903},{8... | collective-permute-start | bytes 1572872 | tf_op jit(solution)/shard_map/ppermute | solution.py:86
  116.6 8.1 %collective-permute-done.10.rest_7_ = bf16[256,1024]{1,0:T(8,128)(2,1)S(1)} collective-permute-done((bf16[256,1024]{1,0:T(8,128)(2,1)S(1)}, bf16[256,1024]{1,0:T(8,128)(2,1)S(1)}, u32[]{:S(2)}, u32[]{:S(2)}) %collective-permute-start.10) | collective-permute-done | bytes 524320 | tf_op jit(solution)/shard_map/ppermute | solution.py:86
  124.7 3.8 %first.1 = (bf16[1024,384]{1,0:T(8,128)(2,1)S(1)}, bf16[2048,1024]{1,0:T(8,128)(2,1)S(1)}) custom-call(bf16[2048,384]{1,0:T(8,128)(2,1)S(1)} %assemble.1.rows_ref, bf16[256,1024]{1,0:T(8,128)(2,1)S(1)} %bitcast.11, bf16[256,1024]{1,0:T(8,128)(2,1)} %copy-done.2, bf16[256,1024]{1,0:T(8,128)(2,1)} %copy-done.1, bf16[256,1024]{1,0:T(8,128)(2,1)} %copy-done.3, ...), custom_call_target="tpu_custom_call" | custom-call | tf_op jit(solution)/shard_map/first/pallas_call | solution.py:212
  128.5 3.8 %second.1 = bf16[1024,768]{1,0:T(8,128)(2,1)} custom-call(s32[3]{0:T(128)S(1)} %pad_add_fusion.refs_0_.where_ref, bf16[2048,384]{1,0:T(8,128)(2,1)S(1)} %collective-permute-done.3.rows_ref, bf16[2048,1024]{1,0:T(8,128)(2,1)S(1)} %get-tuple-element.7.hidden_ref, bf16[1024,384]{1,0:T(8,128)(2,1)S(1)} %get-tuple-element.8.done_ref), custom_call_target="tpu_custom_call" | custom-call | tf_op jit(solution)/shard_map/second/pallas_call | solution.py:223
  (17 shorter events, 0.7 us)
Async XLA Ops:
  0.0 52.6 %copy-start = (bf16[1,256,1024]{2,1,0:T(8,128)(2,1)S(1)}, bf16[1,256,1024]{2,1,0:T(8,128)(2,1)}, u32[]{:S(2)}) copy-start(bf16[1,256,1024]{2,1,0:T(8,128)(2,1)} %param.7) | copy-start | bytes 1572868
  45.3 18.0 %all-to-all-start.2 = ((bf16[8,2,32,384]{3,2,1,0:T(8,128)(2,1)}), bf16[8,2,32,384]{3,2,1,0:T(8,128)(2,1)S(1)}, u32[]{:S(2)}, u32[]{:S(2)}) async-start(bf16[8,2,32,384]{3,2,1,0:T(8,128)(2,1)} %all_to_all.16), calls=%async_computation.2 | async-start | bytes 786432 | tf_op jit(solution)/shard_map/all_to_all | solution.py:195
  52.6 20.5 %collective-permute-start.5 = (bf16[256,1024]{1,0:T(8,128)(2,1)S(1)}, bf16[256,1024]{1,0:T(8,128)(2,1)S(1)}, u32[]{:S(2)}, u32[]{:S(2)}) collective-permute-start(bf16[256,1024]{1,0:T(8,128)(2,1)S(1)} %bitcast.9), channel_id=1, source_target_pairs={{0,896},{128,0},{256,128},{384,256},{512,384},{640,512},{768,640},... | collective-permute-start | bytes 1572872 | tf_op jit(solution)/shard_map/ppermute | solution.py:78
  57.2 20.2 %collective-permute-start.4 = (bf16[256,1024]{1,0:T(8,128)(2,1)S(1)}, bf16[256,1024]{1,0:T(8,128)(2,1)S(1)}, u32[]{:S(2)}, u32[]{:S(2)}) collective-permute-start(bf16[256,1024]{1,0:T(8,128)(2,1)S(1)} %bitcast.10), channel_id=1, source_target_pairs={{0,128},{128,256},{256,384},{384,512},{512,640},{640,768},{768,896... | collective-permute-start | bytes 1572872 | tf_op jit(solution)/shard_map/ppermute | solution.py:77
  63.4 16.0 %collective-permute-start.2 = (bf16[8,2,32,384]{3,2,1,0:T(8,128)(2,1)S(1)}, bf16[8,2,32,384]{3,2,1,0:T(8,128)(2,1)S(1)}, u32[]{:S(2)}, u32[]{:S(2)}) collective-permute-start(bf16[8,2,32,384]{3,2,1,0:T(8,128)(2,1)S(1)} %all-to-all-done.2.refs_1_), channel_id=1, source_target_pairs={{0,4},{1,13},{2,6},{3,15},{4,8},{5,1},{6,10},{7,3},{8,12},{9,5},{1... | collective-permute-start | bytes 1179656 | tf_op jit(solution)/shard_map/ppermute | solution.py:198
  67.7 12.5 %collective-permute-start.1 = (bf16[8,2,32,384]{3,2,1,0:T(8,128)(2,1)S(1)}, bf16[8,2,32,384]{3,2,1,0:T(8,128)(2,1)S(1)}, u32[]{:S(2)}, u32[]{:S(2)}) collective-permute-start(bf16[8,2,32,384]{3,2,1,0:T(8,128)(2,1)S(1)} %all-to-all-done.2.refs_1_), channel_id=1, source_target_pairs={{0,14},{1,15},{2,0},{3,1},{4,2},{5,3},{6,4},{7,5},{8,6},{9,7},{10,... | collective-permute-start | bytes 1179656 | tf_op jit(solution)/shard_map/ppermute | solution.py:197
  69.6 16.3 %collective-permute-start = (bf16[8,2,32,384]{3,2,1,0:T(8,128)(2,1)S(1)}, bf16[8,2,32,384]{3,2,1,0:T(8,128)(2,1)S(1)}, u32[]{:S(2)}, u32[]{:S(2)}) collective-permute-start(bf16[8,2,32,384]{3,2,1,0:T(8,128)(2,1)S(1)} %all-to-all-done.2.refs_1_), channel_id=1, source_target_pairs={{0,2},{1,3},{2,4},{3,5},{4,6},{5,7},{6,8},{7,9},{8,10},{9,11},{10,... | collective-permute-start | bytes 1179656 | tf_op jit(solution)/shard_map/ppermute | solution.py:196
  73.1 13.6 %copy-start.1 = (bf16[256,1024]{1,0:T(8,128)(2,1)}, bf16[256,1024]{1,0:T(8,128)(2,1)S(1)}, u32[]{:S(2)}) copy-start(bf16[256,1024]{1,0:T(8,128)(2,1)S(1)} %collective-permute-done.5.rest_2_) | copy-start | bytes 1572868
  73.1 22.2 %collective-permute-start.7 = (bf16[256,1024]{1,0:T(8,128)(2,1)S(1)}, bf16[256,1024]{1,0:T(8,128)(2,1)S(1)}, u32[]{:S(2)}, u32[]{:S(2)}) collective-permute-start(bf16[256,1024]{1,0:T(8,128)(2,1)S(1)} %collective-permute-done.5.rest_2_), channel_id=1, source_target_pairs={{0,896},{128,0},{256,128},{384,256},{512,384},{640,512},{768,640},... | collective-permute-start | bytes 1572872 | tf_op jit(solution)/shard_map/ppermute | solution.py:78
  77.4 9.3 %copy-start.2 = (bf16[256,1024]{1,0:T(8,128)(2,1)}, bf16[256,1024]{1,0:T(8,128)(2,1)S(1)}, u32[]{:S(2)}) copy-start(bf16[256,1024]{1,0:T(8,128)(2,1)S(1)} %collective-permute-done.4.rest_1_) | copy-start | bytes 1572868
  77.4 19.9 %collective-permute-start.6 = (bf16[256,1024]{1,0:T(8,128)(2,1)S(1)}, bf16[256,1024]{1,0:T(8,128)(2,1)S(1)}, u32[]{:S(2)}, u32[]{:S(2)}) collective-permute-start(bf16[256,1024]{1,0:T(8,128)(2,1)S(1)} %collective-permute-done.4.rest_1_), channel_id=1, source_target_pairs={{0,128},{128,256},{256,384},{384,512},{512,640},{640,768},{768,896... | collective-permute-start | bytes 1572872 | tf_op jit(solution)/shard_map/ppermute | solution.py:77
  86.7 41.8 %collective-permute-start.3 = (bf16[2048,384]{1,0:T(8,128)(2,1)S(1)}, bf16[2048,384]{1,0:T(8,128)(2,1)S(1)}, u32[]{:S(2)}, u32[]{:S(2)}) collective-permute-start(bf16[2048,384]{1,0:T(8,128)(2,1)S(1)} %assemble.1.rows_ref), channel_id=1, source_target_pairs={{0,1},{1,0},{2,3},{3,2},{4,5},{5,4},{6,7},{7,6},{8,9},{9,8},{10,11... | collective-permute-start | bytes 4718600 | tf_op jit(solution)/shard_map/ppermute | solution.py:209
  95.4 15.4 %collective-permute-start.9 = (bf16[256,1024]{1,0:T(8,128)(2,1)S(1)}, bf16[256,1024]{1,0:T(8,128)(2,1)S(1)}, u32[]{:S(2)}, u32[]{:S(2)}) collective-permute-start(bf16[256,1024]{1,0:T(8,128)(2,1)S(1)} %collective-permute-done.7.rest_4_), channel_id=1, source_target_pairs={{0,896},{128,0},{256,128},{384,256},{512,384},{640,512},{768,640},... | collective-permute-start | bytes 1572872 | tf_op jit(solution)/shard_map/ppermute | solution.py:78
  97.3 27.4 %copy-start.3 = (bf16[256,1024]{1,0:T(8,128)(2,1)}, bf16[256,1024]{1,0:T(8,128)(2,1)S(1)}, u32[]{:S(2)}) copy-start(bf16[256,1024]{1,0:T(8,128)(2,1)S(1)} %collective-permute-done.6.rest_3_) | copy-start | bytes 1572868
  97.3 16.6 %collective-permute-start.8 = (bf16[256,1024]{1,0:T(8,128)(2,1)S(1)}, bf16[256,1024]{1,0:T(8,128)(2,1)S(1)}, u32[]{:S(2)}, u32[]{:S(2)}) collective-permute-start(bf16[256,1024]{1,0:T(8,128)(2,1)S(1)} %collective-permute-done.6.rest_3_), channel_id=1, source_target_pairs={{0,128},{128,256},{256,384},{384,512},{512,640},{640,768},{768,896... | collective-permute-start | bytes 1572872 | tf_op jit(solution)/shard_map/ppermute | solution.py:77
  114.5 10.2 %collective-permute-start.10 = (bf16[256,1024]{1,0:T(8,128)(2,1)S(1)}, bf16[256,1024]{1,0:T(8,128)(2,1)S(1)}, u32[]{:S(2)}, u32[]{:S(2)}) collective-permute-start(bf16[256,1024]{1,0:T(8,128)(2,1)S(1)} %pick.1), channel_id=1, source_target_pairs={{0,128},{1,897},{2,130},{3,899},{4,132},{5,901},{6,134},{7,903},{8... | collective-permute-start | bytes 1572872 | tf_op jit(solution)/shard_map/ppermute | solution.py:86

commit v4 on v3

--- a/solution.py
+++ b/solution.py
@@ -42,26 +42,28 @@
         out_ref[e] = (picked * weight).astype(out_ref.dtype)
 
 
-def pick_body(where_ref, even_ref, odd_ref, out_ref):
-    @pl.when(where_ref[2] == 0)
+def pick_body(even_ref, odd_ref, out_ref):
+    core = lax.axis_index("tensor") % CORES
+
+    @pl.when(core == 0)
     def _():
         out_ref[...] = even_ref[...]
 
-    @pl.when(where_ref[2] != 0)
+    @pl.when(core != 0)
     def _():
         out_ref[...] = odd_ref[...]
 
 
-def pick(place, even, odd):
+def pick(even, odd):
     vmem = pl.BlockSpec(memory_space=pltpu.VMEM)
     return pl.pallas_call(
         pick_body,
         out_shape=pltpu.VMEM(even.shape, even.dtype),
-        in_specs=[pl.BlockSpec(memory_space=pltpu.SMEM), vmem, vmem],
+        in_specs=[vmem, vmem],
         out_specs=vmem,
         compiler_params=pltpu.CompilerParams(vmem_limit_bytes=2 << 20),
         name="pick",
-    )(place, in_vmem(even), in_vmem(odd))
+    )(in_vmem(even), in_vmem(odd))
 
 
 def twice_body(in_ref, out_ref):
@@ -69,7 +71,7 @@
         out_ref[k] = in_ref[...]
 
 
-def hidden_ring(hidden, place, count, tensor_count):
+def hidden_ring(hidden, count, tensor_count):
     up = [(k, (k + 1) % count) for k in range(count)]
     down = [(k, (k - 1) % count) for k in range(count)]
     below, above, pieces = hidden, hidden, [hidden]
@@ -82,18 +84,18 @@
         for y in range(count)
         for t in range(tensor_count)
     ]
-    last = pick(place, below, above)
+    last = pick(below, above)
     last = lax.ppermute(last, ("dp", "tensor"), across)
     return pieces + [last]
 
 
-def assemble_body(count, where_ref, *refs):
-    me, mine = where_ref[0], where_ref[1]
+def assemble_body(count, *refs):
+    me, chip = lax.axis_index("dp"), lax.axis_index("tensor") // CORES
     own_ref, below_ref, above_ref, far_ref, out_ref = refs
     groups = count // 2
     size = own_ref.shape[1] * own_ref.shape[2]
     for step, ref in ((0, own_ref), (-1, below_ref), (1, above_ref), (2, far_ref)):
-        row = ((mine + step) % groups) * size
+        row = ((chip + step) % groups) * size
         for i in range(count):
             ahead = (i - me) % count
             place = jnp.where(
@@ -106,52 +108,57 @@
                 out_ref[pl.ds(pl.multiple_of(start, CAP), CAP), :] = ref[i, part]
 
 
-def products(hidden_ref, rows_ref):
-    block = hidden_ref.shape[1] // 4
-    for g in range(4):
-        units = slice(g * block, (g + 1) * block)
-        yield units, lax.dot_general(
-            hidden_ref[:, units],
-            rows_ref[...],
-            (((0,), (0,)), ((), ())),
-            preferred_element_type=jnp.float32,
-        )
+def product(hidden, rows):
+    return lax.dot_general(
+        hidden, rows, (((0,), (0,)), ((), ())), preferred_element_type=jnp.float32
+    )
+
+
+def blocks(size):
+    return [slice(g * size // 4, (g + 1) * size // 4) for g in range(4)]
 
 
 def first_body(rows_ref, *rest):
-    piece_refs, out_ref, hidden_ref = rest[:-2], *rest[-2:]
+    piece_refs, part_ref, hidden_ref = rest[:-2], *rest[-2:]
     at = 0
     for ref in piece_refs:
         hidden_ref[at : at + ref.shape[0], :] = ref[...]
         at += ref.shape[0]
-    for units, total in products(hidden_ref, rows_ref):
-        out_ref[units, :] = total.astype(out_ref.dtype)
-
-
-def second_body(where_ref, rows_ref, hidden_ref, done_ref, out_ref, block_ref, sems):
-    width, core = rows_ref.shape[-1], where_ref[2]
-    own = pl.ds(pl.multiple_of(core * width, 128), width)
-    rest = pl.ds(pl.multiple_of((1 - core) * width, 128), width)
-    copies = [pltpu.make_async_copy(done_ref, out_ref.at[:, own], sems.at[0])]
-    copies[0].start()
-    for units, total in products(hidden_ref, rows_ref):
-        block_ref[units, :] = total.astype(block_ref.dtype)
+    for units in blocks(part_ref.shape[0]):
+        part_ref[units, :] = product(hidden_ref[:, units], rows_ref[:at, :])
+
+
+def second_body(
+    mine_ref, other_ref, hidden_ref, last_ref, part_ref, out_ref, own_ref, rest_ref, sems
+):
+    width, core = mine_ref.shape[-1], lax.axis_index("tensor") % CORES
+    early = hidden_ref.shape[0]
+    columns = [pl.ds(pl.multiple_of(c * width, 128), width) for c in (core, 1 - core)]
+    copies = []
+
+    def send(ref, units, column):
         copies.append(
             pltpu.make_async_copy(
-                block_ref.at[units], out_ref.at[units, rest], sems.at[len(copies)]
+                ref.at[units], out_ref.at[units, column], sems.at[len(copies)]
             )
         )
         copies[-1].start()
+
+    for units in blocks(part_ref.shape[0]):
+        total = part_ref[units, :] + product(last_ref[:, units], mine_ref[early:, :])
+        own_ref[units, :] = total.astype(own_ref.dtype)
+        send(own_ref, units, columns[0])
+    for units in blocks(part_ref.shape[0]):
+        total = product(hidden_ref[:, units], other_ref[:early, :])
+        total += product(last_ref[:, units], other_ref[early:, :])
+        rest_ref[units, :] = total.astype(rest_ref.dtype)
+        send(rest_ref, units, columns[1])
     for copy in copies:
         copy.wait()
 
 
 def in_vmem(array):
     return pltpu.with_memory_space_constraint(array, pltpu.VMEM)
-
-
-def in_hbm(array):
-    return pltpu.with_memory_space_constraint(array, pltpu.HBM)
 
 
 def local(grad_out, expert_ids, route_gates, saved_hidden):
@@ -169,12 +176,9 @@
 
     swap = [(k, k ^ 1) for k in range(tensor_count)]
     same_core = [[c + CORES * k for k in range(chips)] for c in range(CORES)]
-    smem = pl.BlockSpec(memory_space=pltpu.SMEM)
     vmem = pl.BlockSpec(memory_space=pltpu.VMEM)
 
-    t = lax.axis_index("tensor")
-    place = jnp.stack([lax.axis_index("dp"), t // CORES % groups, t % CORES]).astype(jnp.int32)
-    pieces = hidden_ring(hidden, place, data_count, tensor_count)
+    pieces = hidden_ring(hidden, data_count, tensor_count)
 
     slots = pl.pallas_call(
         lambda *refs: select_body(expert_count, *refs),
@@ -198,37 +202,42 @@
     far = lax.ppermute(slots, "tensor", shift(2 * CORES, -2 * CORES))
 
     taken = data_count * rows
+    early = taken - rows
     mine = pl.pallas_call(
         lambda *refs: assemble_body(data_count, *refs),
         out_shape=pltpu.VMEM((taken, width), jnp.bfloat16),
-        in_specs=[smem] + [vmem] * 4,
+        in_specs=[vmem] * 4,
         out_specs=vmem,
         compiler_params=pltpu.CompilerParams(vmem_limit_bytes=4 << 20),
         name="assemble",
-    )(place, *[in_vmem(p) for p in (slots, below, above, far)])
+    )(*[in_vmem(p) for p in (slots, below, above, far)])
     other = lax.ppermute(mine, "tensor", swap)
 
     params = pltpu.CompilerParams(vmem_limit_bytes=14 << 20)
-    done, gathered = pl.pallas_call(
+    part, gathered = pl.pallas_call(
         first_body,
         out_shape=(
-            pltpu.VMEM((units, width), jnp.bfloat16),
-            pltpu.VMEM((taken, units), jnp.bfloat16),
+            pltpu.VMEM((units, width), jnp.float32),
+            pltpu.VMEM((early, units), jnp.bfloat16),
         ),
-        in_specs=[vmem] * (1 + len(pieces)),
+        in_specs=[vmem] * len(pieces),
         out_specs=(vmem, vmem),
         compiler_params=params,
         name="first",
-    )(in_vmem(mine), *[in_hbm(p) if n in (1, 2, 3) else p for n, p in enumerate(pieces)])
+    )(in_vmem(mine), *pieces[:-1])
     out = pl.pallas_call(
         second_body,
         out_shape=jax.ShapeDtypeStruct((units, CORES * width), jnp.bfloat16),
-        in_specs=[smem] + [vmem] * 3,
+        in_specs=[vmem] * 5,
         out_specs=pl.BlockSpec(memory_space=pl.ANY),
-        scratch_shapes=[pltpu.VMEM((units, width), jnp.bfloat16), pltpu.SemaphoreType.DMA((5,))],
+        scratch_shapes=[
+            pltpu.VMEM((units, width), jnp.bfloat16),
+            pltpu.VMEM((units, width), jnp.bfloat16),
+            pltpu.SemaphoreType.DMA((8,)),
+        ],
         compiler_params=params,
         name="second",
-    )(place, in_vmem(other), in_vmem(gathered), in_vmem(done))
+    )(*[in_vmem(a) for a in (mine, other, gathered, pieces[-1], part)])
     return out[None]
 
 

time: 133 us -> 128 us (0.962)
  waiting for transfers between devices: 32.2 us -> 27.8 us
  Pallas kernels: 10.2 us -> 7.19 us
  starting transfers between devices: 45.6 us -> 48.2 us
    ppermute x3, waiting for transfers between devices: 10 us -> 0.92 us  [hidden_ring(): above = lax.ppermute(above, 'dp', down)]
    ppermute x3, waiting for transfers between devices: 3.16 us -> 10.9 us  [hidden_ring(): below = lax.ppermute(below, 'dp', up)]
    ppermute x1, waiting for transfers between devices: 0.01 us -> 7.69 us  [local(): far = lax.ppermute(slots, 'tensor', shift(2 * CORES, -2 * CORES))]
    ppermute x1, waiting for transfers between devices: 5.72 us -> 0.01 us  [local(): below = lax.ppermute(slots, 'tensor', shift(CORES))]
    ppermute x1, waiting for transfers between devices: 8.08 us -> 3.95 us  [hidden_ring(): last = lax.ppermute(last, ('dp', 'tensor'), across)]
    ppermute x1, starting transfers between devices: 2.13 us -> 5.32 us  [hidden_ring(): last = lax.ppermute(last, ('dp', 'tensor'), across)]
    ppermute x1, starting transfers between devices: 1.92 us -> 4.57 us  [local(): above = lax.ppermute(slots, 'tensor', shift(-CORES))]
    ppermute x1, starting transfers between devices: 8.64 us -> 6.81 us  [local(): other = lax.ppermute(mine, 'tensor', swap)]
  transfers between devices with their start and end apart: 12 -> 12, of which waited for: 6 -> 6; matrix products, arithmetic and copies ran while one was open for 0% -> 0% of each run, Pallas kernels for 4% -> 2%
where the time goes in v4:
time: 128 us; the launch traced here: 127 us
  starting transfers between devices  48.2 us (38%)
  blocking collectives  43.9 us (34%)
  waiting for transfers between devices  27.8 us (22%)
  Pallas kernels  7.19 us (6%)
    all_to_all x1, blocking collectives, local(): slots = lax.all_to_all(slots, 'expert', 0, 0, tiled=True)  26 us
    all_to_all x1, blocking collectives, local(): lax.all_to_all(slots, 'tensor', 0, 0, tiled=True, axis_index_groups=same_...  17.9 us
    ppermute x3, starting transfers between devices, hidden_ring(): above = lax.ppermute(above, 'dp', down)  12.2 us
    ppermute x3, waiting for transfers between devices, hidden_ring(): below = lax.ppermute(below, 'dp', up)  10.9 us
    ppermute x1, waiting for transfers between devices, local(): far = lax.ppermute(slots, 'tensor', shift(2 * CORES, -2 * CORES))  7.69 us
    all_to_all x1, starting transfers between devices, local(): slots = lax.all_to_all(slots, 'dp', 0, 0, tiled=True)  7.28 us
    ppermute x3, starting transfers between devices, hidden_ring(): below = lax.ppermute(below, 'dp', up)  7.27 us
    ppermute x1, starting transfers between devices, local(): other = lax.ppermute(mine, 'tensor', swap)  6.81 us
  transfers between devices with their start and end apart: 12, of which 6 were waited for; matrix products, arithmetic and copies ran while one was open for 0% of the time, Pallas kernels for 2%

profile of v4, /device:TPU:1, one launch (start us, length us, event | category | flops | bytes accessed | tf_op | source)
XLA Modules:
  0.0 127.3 jit_solution(11237650742122879421)
XLA Ops:
  0.0 1.4 %select.1 = bf16[8,32,384]{2,1,0:T(8,128)(2,1)S(1)} custom-call(s32[2,128]{1,0:T(2,128)} %bitcast.9, f32[2,128]{1,0:T(2,128)} %bitcast.10, bf16[128,384]{1,0:T(8,128)(2,1)} %refs_2_.1), custom_call_target="tpu_custom_call" | custom-call | tf_op jit(solution)/shard_map/select/pallas_call | solution.py:183
  1.4 26.0 %all_to_all.15.in_ref = bf16[8,32,384]{2,1,0:T(8,128)(2,1)S(1)} all-to-all(bf16[8,32,384]{2,1,0:T(8,128)(2,1)S(1)} %select.1), channel_id=1, replica_groups=mesh['dp'=8,'expert'=8,'tensor'=16] {'expert'}, dimensions={0} | all-to-all | bytes 393216 | tf_op jit(solution)/shard_map/all_to_all | solution.py:188
  27.4 17.9 %all_to_all.16 = bf16[8,2,32,384]{3,2,1,0:T(8,128)(2,1)} all-to-all(bf16[8,2,32,384]{3,2,1,0:T(8,128)(2,1)S(1)} %bitcast.5), channel_id=1, replica_groups={{0,2,4,6,8,10,12,14},{1,3,5,7,9,11,13,15},{16,18,20,22,24,26,28,30},{17..., dimensions={0} | all-to-all | bytes 786432 | tf_op jit(solution)/shard_map/all_to_all | solution.py:198
  45.3 7.3 %all-to-all-start.2 = ((bf16[8,2,32,384]{3,2,1,0:T(8,128)(2,1)}), bf16[8,2,32,384]{3,2,1,0:T(8,128)(2,1)S(1)}, u32[]{:S(2)}, u32[]{:S(2)}) async-start(bf16[8,2,32,384]{3,2,1,0:T(8,128)(2,1)} %all_to_all.16), calls=%async_computation.2 | async-start | bytes 786432 | tf_op jit(solution)/shard_map/all_to_all | solution.py:199
  52.6 3.4 %collective-permute-start.4 = (bf16[256,1024]{1,0:T(8,128)(2,1)S(1)}, bf16[256,1024]{1,0:T(8,128)(2,1)S(1)}, u32[]{:S(2)}, u32[]{:S(2)}) collective-permute-start(bf16[256,1024]{1,0:T(8,128)(2,1)S(1)} %bitcast.6), channel_id=1, source_target_pairs={{0,128},{128,256},{256,384},{384,512},{512,640},{640,768},{768,896... | collective-permute-start | bytes 1572872 | tf_op jit(solution)/shard_map/ppermute | solution.py:79
  56.0 3.1 %collective-permute-start.5 = (bf16[256,1024]{1,0:T(8,128)(2,1)S(1)}, bf16[256,1024]{1,0:T(8,128)(2,1)S(1)}, u32[]{:S(2)}, u32[]{:S(2)}) collective-permute-start(bf16[256,1024]{1,0:T(8,128)(2,1)S(1)} %bitcast.7), channel_id=1, source_target_pairs={{0,896},{128,0},{256,128},{384,256},{512,384},{640,512},{768,640},... | collective-permute-start | bytes 1572872 | tf_op jit(solution)/shard_map/ppermute | solution.py:80
  59.1 4.3 %all-to-all-done.2.refs_0_ = bf16[8,2,32,384]{3,2,1,0:T(8,128)(2,1)S(1)} async-done(((bf16[8,2,32,384]{3,2,1,0:T(8,128)(2,1)}), bf16[8,2,32,384]{3,2,1,0:T(8,128)(2,1)S(1)}, u32[]{:S(2)}, u32[]{:S(2)}) %all-to-all-start.2) | async-done | bytes 393248 | tf_op jit(solution)/shard_map/all_to_all | solution.py:199
  63.4 1.9 %collective-permute-start = (bf16[8,2,32,384]{3,2,1,0:T(8,128)(2,1)S(1)}, bf16[8,2,32,384]{3,2,1,0:T(8,128)(2,1)S(1)}, u32[]{:S(2)}, u32[]{:S(2)}) collective-permute-start(bf16[8,2,32,384]{3,2,1,0:T(8,128)(2,1)S(1)} %all-to-all-done.2.refs_0_), channel_id=1, source_target_pairs={{0,2},{1,3},{2,4},{3,5},{4,6},{5,7},{6,8},{7,9},{8,10},{9,11},{10,... | collective-permute-start | bytes 1179656 | tf_op jit(solution)/shard_map/ppermute | solution.py:200
  65.4 4.6 %collective-permute-start.1 = (bf16[8,2,32,384]{3,2,1,0:T(8,128)(2,1)S(1)}, bf16[8,2,32,384]{3,2,1,0:T(8,128)(2,1)S(1)}, u32[]{:S(2)}, u32[]{:S(2)}) collective-permute-start(bf16[8,2,32,384]{3,2,1,0:T(8,128)(2,1)S(1)} %all-to-all-done.2.refs_0_), channel_id=1, source_target_pairs={{0,14},{1,15},{2,0},{3,1},{4,2},{5,3},{6,4},{7,5},{8,6},{9,7},{10,... | collective-permute-start | bytes 1179656 | tf_op jit(solution)/shard_map/ppermute | solution.py:201
  69.9 2.8 %collective-permute-start.2 = (bf16[8,2,32,384]{3,2,1,0:T(8,128)(2,1)S(1)}, bf16[8,2,32,384]{3,2,1,0:T(8,128)(2,1)S(1)}, u32[]{:S(2)}, u32[]{:S(2)}) collective-permute-start(bf16[8,2,32,384]{3,2,1,0:T(8,128)(2,1)S(1)} %all-to-all-done.2.refs_0_), channel_id=1, source_target_pairs={{0,4},{1,13},{2,6},{3,15},{4,8},{5,1},{6,10},{7,3},{8,12},{9,5},{1... | collective-permute-start | bytes 1179656 | tf_op jit(solution)/shard_map/ppermute | solution.py:202
  72.8 0.8 collective-permute-done.4.rest_1_
  73.6 1.9 %collective-permute-start.6 = (bf16[256,1024]{1,0:T(8,128)(2,1)S(1)}, bf16[256,1024]{1,0:T(8,128)(2,1)S(1)}, u32[]{:S(2)}, u32[]{:S(2)}) collective-permute-start(bf16[256,1024]{1,0:T(8,128)(2,1)S(1)} %collective-permute-done.4.rest_1_), channel_id=1, source_target_pairs={{0,128},{128,256},{256,384},{384,512},{512,640},{640,768},{768,896... | collective-permute-start | bytes 1572872 | tf_op jit(solution)/shard_map/ppermute | solution.py:79
  75.6 4.6 %collective-permute-start.7 = (bf16[256,1024]{1,0:T(8,128)(2,1)S(1)}, bf16[256,1024]{1,0:T(8,128)(2,1)S(1)}, u32[]{:S(2)}, u32[]{:S(2)}) collective-permute-start(bf16[256,1024]{1,0:T(8,128)(2,1)S(1)} %collective-permute-done.5.rest_2_), channel_id=1, source_target_pairs={{0,896},{128,0},{256,128},{384,256},{512,384},{640,512},{768,640},... | collective-permute-start | bytes 1572872 | tf_op jit(solution)/shard_map/ppermute | solution.py:80
  80.2 7.7 %collective-permute-done.2.refs_3_ = bf16[8,2,32,384]{3,2,1,0:T(8,128)(2,1)S(1)} collective-permute-done((bf16[8,2,32,384]{3,2,1,0:T(8,128)(2,1)S(1)}, bf16[8,2,32,384]{3,2,1,0:T(8,128)(2,1)S(1)}, u32[]{:S(2)}, u32[]{:S(2)}) %collective-permute-start.2) | collective-permute-done | bytes 393248 | tf_op jit(solution)/shard_map/ppermute | solution.py:202
  87.9 0.2 assemble.1.rows_ref.mine_ref
  88.1 6.8 %collective-permute-start.3 = (bf16[2048,384]{1,0:T(8,128)(2,1)S(1)}, bf16[2048,384]{1,0:T(8,128)(2,1)S(1)}, u32[]{:S(2)}, u32[]{:S(2)}) collective-permute-start(bf16[2048,384]{1,0:T(8,128)(2,1)S(1)} %assemble.1.rows_ref.mine_ref), channel_id=1, source_target_pairs={{0,1},{1,0},{2,3},{3,2},{4,5},{5,4},{6,7},{7,6},{8,9},{9,8},{10,11... | collective-permute-start | bytes 4718600 | tf_op jit(solution)/shard_map/ppermute | solution.py:214
  94.9 2.0 %collective-permute-start.8 = (bf16[256,1024]{1,0:T(8,128)(2,1)S(1)}, bf16[256,1024]{1,0:T(8,128)(2,1)S(1)}, u32[]{:S(2)}, u32[]{:S(2)}) collective-permute-start(bf16[256,1024]{1,0:T(8,128)(2,1)S(1)} %collective-permute-done.6.rest_3_), channel_id=1, source_target_pairs={{0,128},{128,256},{256,384},{384,512},{512,640},{640,768},{768,896... | collective-permute-start | bytes 1572872 | tf_op jit(solution)/shard_map/ppermute | solution.py:79
  96.9 4.5 %collective-permute-start.9 = (bf16[256,1024]{1,0:T(8,128)(2,1)S(1)}, bf16[256,1024]{1,0:T(8,128)(2,1)S(1)}, u32[]{:S(2)}, u32[]{:S(2)}) collective-permute-start(bf16[256,1024]{1,0:T(8,128)(2,1)S(1)} %collective-permute-done.7.rest_4_), channel_id=1, source_target_pairs={{0,896},{128,0},{256,128},{384,256},{512,384},{640,512},{768,640},... | collective-permute-start | bytes 1572872 | tf_op jit(solution)/shard_map/ppermute | solution.py:80
  101.4 10.1 %collective-permute-done.8.rest_5_.even_ref = bf16[256,1024]{1,0:T(8,128)(2,1)S(1)} collective-permute-done((bf16[256,1024]{1,0:T(8,128)(2,1)S(1)}, bf16[256,1024]{1,0:T(8,128)(2,1)S(1)}, u32[]{:S(2)}, u32[]{:S(2)}) %collective-permute-start.8) | collective-permute-done | bytes 524320 | tf_op jit(solution)/shard_map/ppermute | solution.py:79
  111.5 0.9 collective-permute-done.9.rest_6_.odd_ref
  112.4 5.3 %collective-permute-start.10 = (bf16[256,1024]{1,0:T(8,128)(2,1)S(1)}, bf16[256,1024]{1,0:T(8,128)(2,1)S(1)}, u32[]{:S(2)}, u32[]{:S(2)}) collective-permute-start(bf16[256,1024]{1,0:T(8,128)(2,1)S(1)} %pick.1), channel_id=1, source_target_pairs={{0,128},{1,897},{2,130},{3,899},{4,132},{5,901},{6,134},{7,903},{8... | collective-permute-start | bytes 1572872 | tf_op jit(solution)/shard_map/ppermute | solution.py:88
  117.7 2.1 %first.1 = (f32[1024,384]{1,0:T(8,128)S(1)}, bf16[1792,1024]{1,0:T(8,128)(2,1)S(1)}) custom-call(bf16[2048,384]{1,0:T(8,128)(2,1)S(1)} %assemble.1.rows_ref.mine_ref, bf16[256,1024]{1,0:T(8,128)(2,1)S(1)} %bitcast.8, bf16[256,1024]{1,0:T(8,128)(2,1)S(1)} %collective-permute-done.4.rest_1_, bf16[256,1024]{1,0:T(8,128)(2,1)S(1)} %collective-permute-done.5.rest_2_, ...), custom_call_target="tpu_custom_call" | custom-call | tf_op jit(solution)/shard_map/first/pallas_call | solution.py:217
  119.9 4.0 %collective-permute-done.10.last_ref = bf16[256,1024]{1,0:T(8,128)(2,1)S(1)} collective-permute-done((bf16[256,1024]{1,0:T(8,128)(2,1)S(1)}, bf16[256,1024]{1,0:T(8,128)(2,1)S(1)}, u32[]{:S(2)}, u32[]{:S(2)}) %collective-permute-start.10) | collective-permute-done | bytes 524320 | tf_op jit(solution)/shard_map/ppermute | solution.py:88
  123.8 3.4 %second.1 = bf16[1024,768]{1,0:T(8,128)(2,1)} custom-call(bf16[2048,384]{1,0:T(8,128)(2,1)S(1)} %assemble.1.rows_ref.mine_ref, bf16[2048,384]{1,0:T(8,128)(2,1)S(1)} %collective-permute-done.3.other_ref, bf16[1792,1024]{1,0:T(8,128)(2,1)S(1)} %get-tuple-element.7.hidden_ref, bf16[256,1024]{1,0:T(8,128)(2,1)S(1)} %collective-permute-done.10.last_ref, ...), custom_call_target="tpu_custom_call" | custom-call | tf_op jit(solution)/shard_map/second/pallas_call | solution.py:228
  (10 shorter events, 0.1 us)
Async XLA Ops:
  0.0 52.6 %copy-start = (bf16[1,256,1024]{2,1,0:T(8,128)(2,1)S(1)}, bf16[1,256,1024]{2,1,0:T(8,128)(2,1)}, u32[]{:S(2)}) copy-start(bf16[1,256,1024]{2,1,0:T(8,128)(2,1)} %param.7) | copy-start | bytes 1572868
  45.3 18.1 %all-to-all-start.2 = ((bf16[8,2,32,384]{3,2,1,0:T(8,128)(2,1)}), bf16[8,2,32,384]{3,2,1,0:T(8,128)(2,1)S(1)}, u32[]{:S(2)}, u32[]{:S(2)}) async-start(bf16[8,2,32,384]{3,2,1,0:T(8,128)(2,1)} %all_to_all.16), calls=%async_computation.2 | async-start | bytes 786432 | tf_op jit(solution)/shard_map/all_to_all | solution.py:199
  52.6 21.0 %collective-permute-start.4 = (bf16[256,1024]{1,0:T(8,128)(2,1)S(1)}, bf16[256,1024]{1,0:T(8,128)(2,1)S(1)}, u32[]{:S(2)}, u32[]{:S(2)}) collective-permute-start(bf16[256,1024]{1,0:T(8,128)(2,1)S(1)} %bitcast.6), channel_id=1, source_target_pairs={{0,128},{128,256},{256,384},{384,512},{512,640},{640,768},{768,896... | collective-permute-start | bytes 1572872 | tf_op jit(solution)/shard_map/ppermute | solution.py:79
  56.0 19.6 %collective-permute-start.5 = (bf16[256,1024]{1,0:T(8,128)(2,1)S(1)}, bf16[256,1024]{1,0:T(8,128)(2,1)S(1)}, u32[]{:S(2)}, u32[]{:S(2)}) collective-permute-start(bf16[256,1024]{1,0:T(8,128)(2,1)S(1)} %bitcast.7), channel_id=1, source_target_pairs={{0,896},{128,0},{256,128},{384,256},{512,384},{640,512},{768,640},... | collective-permute-start | bytes 1572872 | tf_op jit(solution)/shard_map/ppermute | solution.py:80
  63.4 16.7 %collective-permute-start = (bf16[8,2,32,384]{3,2,1,0:T(8,128)(2,1)S(1)}, bf16[8,2,32,384]{3,2,1,0:T(8,128)(2,1)S(1)}, u32[]{:S(2)}, u32[]{:S(2)}) collective-permute-start(bf16[8,2,32,384]{3,2,1,0:T(8,128)(2,1)S(1)} %all-to-all-done.2.refs_0_), channel_id=1, source_target_pairs={{0,2},{1,3},{2,4},{3,5},{4,6},{5,7},{6,8},{7,9},{8,10},{9,11},{10,... | collective-permute-start | bytes 1179656 | tf_op jit(solution)/shard_map/ppermute | solution.py:200
  65.4 14.8 %collective-permute-start.1 = (bf16[8,2,32,384]{3,2,1,0:T(8,128)(2,1)S(1)}, bf16[8,2,32,384]{3,2,1,0:T(8,128)(2,1)S(1)}, u32[]{:S(2)}, u32[]{:S(2)}) collective-permute-start(bf16[8,2,32,384]{3,2,1,0:T(8,128)(2,1)S(1)} %all-to-all-done.2.refs_0_), channel_id=1, source_target_pairs={{0,14},{1,15},{2,0},{3,1},{4,2},{5,3},{6,4},{7,5},{8,6},{9,7},{10,... | collective-permute-start | bytes 1179656 | tf_op jit(solution)/shard_map/ppermute | solution.py:201
  69.9 17.9 %collective-permute-start.2 = (bf16[8,2,32,384]{3,2,1,0:T(8,128)(2,1)S(1)}, bf16[8,2,32,384]{3,2,1,0:T(8,128)(2,1)S(1)}, u32[]{:S(2)}, u32[]{:S(2)}) collective-permute-start(bf16[8,2,32,384]{3,2,1,0:T(8,128)(2,1)S(1)} %all-to-all-done.2.refs_0_), channel_id=1, source_target_pairs={{0,4},{1,13},{2,6},{3,15},{4,8},{5,1},{6,10},{7,3},{8,12},{9,5},{1... | collective-permute-start | bytes 1179656 | tf_op jit(solution)/shard_map/ppermute | solution.py:202
  73.6 21.2 %collective-permute-start.6 = (bf16[256,1024]{1,0:T(8,128)(2,1)S(1)}, bf16[256,1024]{1,0:T(8,128)(2,1)S(1)}, u32[]{:S(2)}, u32[]{:S(2)}) collective-permute-start(bf16[256,1024]{1,0:T(8,128)(2,1)S(1)} %collective-permute-done.4.rest_1_), channel_id=1, source_target_pairs={{0,128},{128,256},{256,384},{384,512},{512,640},{640,768},{768,896... | collective-permute-start | bytes 1572872 | tf_op jit(solution)/shard_map/ppermute | solution.py:79
  75.6 21.3 %collective-permute-start.7 = (bf16[256,1024]{1,0:T(8,128)(2,1)S(1)}, bf16[256,1024]{1,0:T(8,128)(2,1)S(1)}, u32[]{:S(2)}, u32[]{:S(2)}) collective-permute-start(bf16[256,1024]{1,0:T(8,128)(2,1)S(1)} %collective-permute-done.5.rest_2_), channel_id=1, source_target_pairs={{0,896},{128,0},{256,128},{384,256},{512,384},{640,512},{768,640},... | collective-permute-start | bytes 1572872 | tf_op jit(solution)/shard_map/ppermute | solution.py:80
  88.1 35.8 %collective-permute-start.3 = (bf16[2048,384]{1,0:T(8,128)(2,1)S(1)}, bf16[2048,384]{1,0:T(8,128)(2,1)S(1)}, u32[]{:S(2)}, u32[]{:S(2)}) collective-permute-start(bf16[2048,384]{1,0:T(8,128)(2,1)S(1)} %assemble.1.rows_ref.mine_ref), channel_id=1, source_target_pairs={{0,1},{1,0},{2,3},{3,2},{4,5},{5,4},{6,7},{7,6},{8,9},{9,8},{10,11... | collective-permute-start | bytes 4718600 | tf_op jit(solution)/shard_map/ppermute | solution.py:214
  94.9 16.6 %collective-permute-start.8 = (bf16[256,1024]{1,0:T(8,128)(2,1)S(1)}, bf16[256,1024]{1,0:T(8,128)(2,1)S(1)}, u32[]{:S(2)}, u32[]{:S(2)}) collective-permute-start(bf16[256,1024]{1,0:T(8,128)(2,1)S(1)} %collective-permute-done.6.rest_3_), channel_id=1, source_target_pairs={{0,128},{128,256},{256,384},{384,512},{512,640},{640,768},{768,896... | collective-permute-start | bytes 1572872 | tf_op jit(solution)/shard_map/ppermute | solution.py:79
  96.9 15.5 %collective-permute-start.9 = (bf16[256,1024]{1,0:T(8,128)(2,1)S(1)}, bf16[256,1024]{1,0:T(8,128)(2,1)S(1)}, u32[]{:S(2)}, u32[]{:S(2)}) collective-permute-start(bf16[256,1024]{1,0:T(8,128)(2,1)S(1)} %collective-permute-done.7.rest_4_), channel_id=1, source_target_pairs={{0,896},{128,0},{256,128},{384,256},{512,384},{640,512},{768,640},... | collective-permute-start | bytes 1572872 | tf_op jit(solution)/shard_map/ppermute | solution.py:80
  112.4 11.4 %collective-permute-start.10 = (bf16[256,1024]{1,0:T(8,128)(2,1)S(1)}, bf16[256,1024]{1,0:T(8,128)(2,1)S(1)}, u32[]{:S(2)}, u32[]{:S(2)}) collective-permute-start(bf16[256,1024]{1,0:T(8,128)(2,1)S(1)} %pick.1), channel_id=1, source_target_pairs={{0,128},{1,897},{2,130},{3,899},{4,132},{5,901},{6,134},{7,903},{8... | collective-permute-start | bytes 1572872 | tf_op jit(solution)/shard_map/ppermute | solution.py:88

commit v5 on v3

--- a/solution.py
+++ b/solution.py
@@ -42,26 +42,28 @@
         out_ref[e] = (picked * weight).astype(out_ref.dtype)
 
 
-def pick_body(where_ref, even_ref, odd_ref, out_ref):
-    @pl.when(where_ref[2] == 0)
+def pick_body(even_ref, odd_ref, out_ref):
+    core = lax.axis_index("tensor") % CORES
+
+    @pl.when(core == 0)
     def _():
         out_ref[...] = even_ref[...]
 
-    @pl.when(where_ref[2] != 0)
+    @pl.when(core != 0)
     def _():
         out_ref[...] = odd_ref[...]
 
 
-def pick(place, even, odd):
+def pick(even, odd):
     vmem = pl.BlockSpec(memory_space=pltpu.VMEM)
     return pl.pallas_call(
         pick_body,
         out_shape=pltpu.VMEM(even.shape, even.dtype),
-        in_specs=[pl.BlockSpec(memory_space=pltpu.SMEM), vmem, vmem],
+        in_specs=[vmem, vmem],
         out_specs=vmem,
         compiler_params=pltpu.CompilerParams(vmem_limit_bytes=2 << 20),
         name="pick",
-    )(place, in_vmem(even), in_vmem(odd))
+    )(in_vmem(even), in_vmem(odd))
 
 
 def twice_body(in_ref, out_ref):
@@ -69,7 +71,7 @@
         out_ref[k] = in_ref[...]
 
 
-def hidden_ring(hidden, place, count, tensor_count):
+def hidden_ring(hidden, count, tensor_count):
     up = [(k, (k + 1) % count) for k in range(count)]
     down = [(k, (k - 1) % count) for k in range(count)]
     below, above, pieces = hidden, hidden, [hidden]
@@ -82,18 +84,18 @@
         for y in range(count)
         for t in range(tensor_count)
     ]
-    last = pick(place, below, above)
+    last = pick(below, above)
     last = lax.ppermute(last, ("dp", "tensor"), across)
     return pieces + [last]
 
 
-def assemble_body(count, where_ref, *refs):
-    me, mine = where_ref[0], where_ref[1]
+def assemble_body(count, *refs):
+    me, chip = lax.axis_index("dp"), lax.axis_index("tensor") // CORES
     own_ref, below_ref, above_ref, far_ref, out_ref = refs
     groups = count // 2
     size = own_ref.shape[1] * own_ref.shape[2]
     for step, ref in ((0, own_ref), (-1, below_ref), (1, above_ref), (2, far_ref)):
-        row = ((mine + step) % groups) * size
+        row = ((chip + step) % groups) * size
         for i in range(count):
             ahead = (i - me) % count
             place = jnp.where(
@@ -128,8 +130,8 @@
         out_ref[units, :] = total.astype(out_ref.dtype)
 
 
-def second_body(where_ref, rows_ref, hidden_ref, done_ref, out_ref, block_ref, sems):
-    width, core = rows_ref.shape[-1], where_ref[2]
+def second_body(rows_ref, hidden_ref, done_ref, out_ref, block_ref, sems):
+    width, core = rows_ref.shape[-1], lax.axis_index("tensor") % CORES
     own = pl.ds(pl.multiple_of(core * width, 128), width)
     rest = pl.ds(pl.multiple_of((1 - core) * width, 128), width)
     copies = [pltpu.make_async_copy(done_ref, out_ref.at[:, own], sems.at[0])]
@@ -150,10 +152,6 @@
     return pltpu.with_memory_space_constraint(array, pltpu.VMEM)
 
 
-def in_hbm(array):
-    return pltpu.with_memory_space_constraint(array, pltpu.HBM)
-
-
 def local(grad_out, expert_ids, route_gates, saved_hidden):
     data_count = lax.axis_size("dp")
     expert_count = lax.axis_size("expert")
@@ -169,12 +167,9 @@
 
     swap = [(k, k ^ 1) for k in range(tensor_count)]
     same_core = [[c + CORES * k for k in range(chips)] for c in range(CORES)]
-    smem = pl.BlockSpec(memory_space=pltpu.SMEM)
     vmem = pl.BlockSpec(memory_space=pltpu.VMEM)
 
-    t = lax.axis_index("tensor")
-    place = jnp.stack([lax.axis_index("dp"), t // CORES % groups, t % CORES]).astype(jnp.int32)
-    pieces = hidden_ring(hidden, place, data_count, tensor_count)
+    pieces = hidden_ring(hidden, data_count, tensor_count)
 
     slots = pl.pallas_call(
         lambda *refs: select_body(expert_count, *refs),
@@ -201,11 +196,11 @@
     mine = pl.pallas_call(
         lambda *refs: assemble_body(data_count, *refs),
         out_shape=pltpu.VMEM((taken, width), jnp.bfloat16),
-        in_specs=[smem] + [vmem] * 4,
+        in_specs=[vmem] * 4,
         out_specs=vmem,
         compiler_params=pltpu.CompilerParams(vmem_limit_bytes=4 << 20),
         name="assemble",
-    )(place, *[in_vmem(p) for p in (slots, below, above, far)])
+    )(*[in_vmem(p) for p in (slots, below, above, far)])
     other = lax.ppermute(mine, "tensor", swap)
 
     params = pltpu.CompilerParams(vmem_limit_bytes=14 << 20)
@@ -219,16 +214,16 @@
         out_specs=(vmem, vmem),
         compiler_params=params,
         name="first",
-    )(in_vmem(mine), *[in_hbm(p) if n in (1, 2, 3) else p for n, p in enumerate(pieces)])
+    )(in_vmem(mine), *pieces)
     out = pl.pallas_call(
         second_body,
         out_shape=jax.ShapeDtypeStruct((units, CORES * width), jnp.bfloat16),
-        in_specs=[smem] + [vmem] * 3,
+        in_specs=[vmem] * 3,
         out_specs=pl.BlockSpec(memory_space=pl.ANY),
         scratch_shapes=[pltpu.VMEM((units, width), jnp.bfloat16), pltpu.SemaphoreType.DMA((5,))],
         compiler_params=params,
         name="second",
-    )(place, in_vmem(other), in_vmem(gathered), in_vmem(done))
+    )(in_vmem(other), in_vmem(gathered), in_vmem(done))
     return out[None]
 
 

time: 133 us -> 130 us (0.977)
  Pallas kernels: 10.2 us -> 7.14 us
    pallas_call x1, Pallas kernels: 3.77 us -> 2.41 us  [local(): pl.pallas_call(first_body, out_shape=(pltpu.VMEM((units, width), jnp.bflo...]
  transfers between devices with their start and end apart: 12 -> 12, of which waited for: 6 -> 6; matrix products, arithmetic and copies ran while one was open for 0% -> 0% of each run, Pallas kernels for 4% -> 2%
where the time goes in v5:
time: 130 us; the launch traced here: 129 us
  starting transfers between devices  45.7 us (35%)
  blocking collectives  43.9 us (34%)
  waiting for transfers between devices  32.2 us (25%)
  Pallas kernels  7.14 us (5%)
    all_to_all x1, blocking collectives, local(): slots = lax.all_to_all(slots, 'expert', 0, 0, tiled=True)  26 us
    all_to_all x1, blocking collectives, local(): lax.all_to_all(slots, 'tensor', 0, 0, tiled=True, axis_index_groups=same_...  17.9 us
    ppermute x3, starting transfers between devices, hidden_ring(): above = lax.ppermute(above, 'dp', down)  10.8 us
    ppermute x3, waiting for transfers between devices, hidden_ring(): above = lax.ppermute(above, 'dp', down)  10.1 us
    ppermute x1, starting transfers between devices, local(): other = lax.ppermute(mine, 'tensor', swap)  8.64 us
    ppermute x1, waiting for transfers between devices, hidden_ring(): last = lax.ppermute(last, ('dp', 'tensor'), across)  8.08 us
    all_to_all x1, starting transfers between devices, local(): slots = lax.all_to_all(slots, 'dp', 0, 0, tiled=True)  7.28 us
    ppermute x3, starting transfers between devices, hidden_ring(): below = lax.ppermute(below, 'dp', up)  7.2 us
  transfers between devices with their start and end apart: 12, of which 6 were waited for; matrix products, arithmetic and copies ran while one was open for 0% of the time, Pallas kernels for 2%

profile of v5, /device:TPU:1, one launch (start us, length us, event | category | flops | bytes accessed | tf_op | source)
XLA Modules:
  0.0 129.1 jit_solution(5653462262912401859)
XLA Ops:
  0.0 1.4 %select.1 = bf16[8,32,384]{2,1,0:T(8,128)(2,1)S(1)} custom-call(s32[2,128]{1,0:T(2,128)} %bitcast.9, f32[2,128]{1,0:T(2,128)} %bitcast.10, bf16[128,384]{1,0:T(8,128)(2,1)} %refs_2_.1), custom_call_target="tpu_custom_call" | custom-call | tf_op jit(solution)/shard_map/select/pallas_call | solution.py:174
  1.4 26.0 %all_to_all.15.in_ref = bf16[8,32,384]{2,1,0:T(8,128)(2,1)S(1)} all-to-all(bf16[8,32,384]{2,1,0:T(8,128)(2,1)S(1)} %select.1), channel_id=1, replica_groups=mesh['dp'=8,'expert'=8,'tensor'=16] {'expert'}, dimensions={0} | all-to-all | bytes 393216 | tf_op jit(solution)/shard_map/all_to_all | solution.py:179
  27.4 17.9 %all_to_all.16 = bf16[8,2,32,384]{3,2,1,0:T(8,128)(2,1)} all-to-all(bf16[8,2,32,384]{3,2,1,0:T(8,128)(2,1)S(1)} %bitcast.5), channel_id=1, replica_groups={{0,2,4,6,8,10,12,14},{1,3,5,7,9,11,13,15},{16,18,20,22,24,26,28,30},{17..., dimensions={0} | all-to-all | bytes 786432 | tf_op jit(solution)/shard_map/all_to_all | solution.py:189
  45.3 7.3 %all-to-all-start.2 = ((bf16[8,2,32,384]{3,2,1,0:T(8,128)(2,1)}), bf16[8,2,32,384]{3,2,1,0:T(8,128)(2,1)S(1)}, u32[]{:S(2)}, u32[]{:S(2)}) async-start(bf16[8,2,32,384]{3,2,1,0:T(8,128)(2,1)} %all_to_all.16), calls=%async_computation.2 | async-start | bytes 786432 | tf_op jit(solution)/shard_map/all_to_all | solution.py:190
  52.6 4.6 %collective-permute-start.5 = (bf16[256,1024]{1,0:T(8,128)(2,1)S(1)}, bf16[256,1024]{1,0:T(8,128)(2,1)S(1)}, u32[]{:S(2)}, u32[]{:S(2)}) collective-permute-start(bf16[256,1024]{1,0:T(8,128)(2,1)S(1)} %bitcast.6), channel_id=1, source_target_pairs={{0,896},{128,0},{256,128},{384,256},{512,384},{640,512},{768,640},... | collective-permute-start | bytes 1572872 | tf_op jit(solution)/shard_map/ppermute | solution.py:80
  57.2 1.9 %collective-permute-start.4 = (bf16[256,1024]{1,0:T(8,128)(2,1)S(1)}, bf16[256,1024]{1,0:T(8,128)(2,1)S(1)}, u32[]{:S(2)}, u32[]{:S(2)}) collective-permute-start(bf16[256,1024]{1,0:T(8,128)(2,1)S(1)} %bitcast.7), channel_id=1, source_target_pairs={{0,128},{128,256},{256,384},{384,512},{512,640},{640,768},{768,896... | collective-permute-start | bytes 1572872 | tf_op jit(solution)/shard_map/ppermute | solution.py:79
  59.1 4.3 %all-to-all-done.2.refs_0_ = bf16[8,2,32,384]{3,2,1,0:T(8,128)(2,1)S(1)} async-done(((bf16[8,2,32,384]{3,2,1,0:T(8,128)(2,1)}), bf16[8,2,32,384]{3,2,1,0:T(8,128)(2,1)S(1)}, u32[]{:S(2)}, u32[]{:S(2)}) %all-to-all-start.2) | async-done | bytes 393248 | tf_op jit(solution)/shard_map/all_to_all | solution.py:190
  63.4 4.3 %collective-permute-start.2 = (bf16[8,2,32,384]{3,2,1,0:T(8,128)(2,1)S(1)}, bf16[8,2,32,384]{3,2,1,0:T(8,128)(2,1)S(1)}, u32[]{:S(2)}, u32[]{:S(2)}) collective-permute-start(bf16[8,2,32,384]{3,2,1,0:T(8,128)(2,1)S(1)} %all-to-all-done.2.refs_0_), channel_id=1, source_target_pairs={{0,4},{1,13},{2,6},{3,15},{4,8},{5,1},{6,10},{7,3},{8,12},{9,5},{1... | collective-permute-start | bytes 1179656 | tf_op jit(solution)/shard_map/ppermute | solution.py:193
  67.7 1.9 %collective-permute-start.1 = (bf16[8,2,32,384]{3,2,1,0:T(8,128)(2,1)S(1)}, bf16[8,2,32,384]{3,2,1,0:T(8,128)(2,1)S(1)}, u32[]{:S(2)}, u32[]{:S(2)}) collective-permute-start(bf16[8,2,32,384]{3,2,1,0:T(8,128)(2,1)S(1)} %all-to-all-done.2.refs_0_), channel_id=1, source_target_pairs={{0,14},{1,15},{2,0},{3,1},{4,2},{5,3},{6,4},{7,5},{8,6},{9,7},{10,... | collective-permute-start | bytes 1179656 | tf_op jit(solution)/shard_map/ppermute | solution.py:192
  69.6 3.4 %collective-permute-start = (bf16[8,2,32,384]{3,2,1,0:T(8,128)(2,1)S(1)}, bf16[8,2,32,384]{3,2,1,0:T(8,128)(2,1)S(1)}, u32[]{:S(2)}, u32[]{:S(2)}) collective-permute-start(bf16[8,2,32,384]{3,2,1,0:T(8,128)(2,1)S(1)} %all-to-all-done.2.refs_0_), channel_id=1, source_target_pairs={{0,2},{1,3},{2,4},{3,5},{4,6},{5,7},{6,8},{7,9},{8,10},{9,11},{10,... | collective-permute-start | bytes 1179656 | tf_op jit(solution)/shard_map/ppermute | solution.py:191
  73.0 4.4 %collective-permute-start.7 = (bf16[256,1024]{1,0:T(8,128)(2,1)S(1)}, bf16[256,1024]{1,0:T(8,128)(2,1)S(1)}, u32[]{:S(2)}, u32[]{:S(2)}) collective-permute-start(bf16[256,1024]{1,0:T(8,128)(2,1)S(1)} %collective-permute-done.5.rest_2_), channel_id=1, source_target_pairs={{0,896},{128,0},{256,128},{384,256},{512,384},{640,512},{768,640},... | collective-permute-start | bytes 1572872 | tf_op jit(solution)/shard_map/ppermute | solution.py:80
  77.4 1.9 %collective-permute-start.6 = (bf16[256,1024]{1,0:T(8,128)(2,1)S(1)}, bf16[256,1024]{1,0:T(8,128)(2,1)S(1)}, u32[]{:S(2)}, u32[]{:S(2)}) collective-permute-start(bf16[256,1024]{1,0:T(8,128)(2,1)S(1)} %collective-permute-done.4.rest_1_), channel_id=1, source_target_pairs={{0,128},{128,256},{256,384},{384,512},{512,640},{640,768},{768,896... | collective-permute-start | bytes 1572872 | tf_op jit(solution)/shard_map/ppermute | solution.py:79
  79.3 0.9 collective-permute-done.1.refs_2_
  80.2 5.7 %collective-permute-done.refs_1_ = bf16[8,2,32,384]{3,2,1,0:T(8,128)(2,1)S(1)} collective-permute-done((bf16[8,2,32,384]{3,2,1,0:T(8,128)(2,1)S(1)}, bf16[8,2,32,384]{3,2,1,0:T(8,128)(2,1)S(1)}, u32[]{:S(2)}, u32[]{:S(2)}) %collective-permute-start) | collective-permute-done | bytes 393248 | tf_op jit(solution)/shard_map/ppermute | solution.py:191
  85.9 0.2 assemble.1.rows_ref
  86.1 8.6 %collective-permute-start.3 = (bf16[2048,384]{1,0:T(8,128)(2,1)S(1)}, bf16[2048,384]{1,0:T(8,128)(2,1)S(1)}, u32[]{:S(2)}, u32[]{:S(2)}) collective-permute-start(bf16[2048,384]{1,0:T(8,128)(2,1)S(1)} %assemble.1.rows_ref), channel_id=1, source_target_pairs={{0,1},{1,0},{2,3},{3,2},{4,5},{5,4},{6,7},{7,6},{8,9},{9,8},{10,11... | collective-permute-start | bytes 4718600 | tf_op jit(solution)/shard_map/ppermute | solution.py:204
  94.8 1.9 %collective-permute-start.9 = (bf16[256,1024]{1,0:T(8,128)(2,1)S(1)}, bf16[256,1024]{1,0:T(8,128)(2,1)S(1)}, u32[]{:S(2)}, u32[]{:S(2)}) collective-permute-start(bf16[256,1024]{1,0:T(8,128)(2,1)S(1)} %collective-permute-done.7.rest_4_), channel_id=1, source_target_pairs={{0,896},{128,0},{256,128},{384,256},{512,384},{640,512},{768,640},... | collective-permute-start | bytes 1572872 | tf_op jit(solution)/shard_map/ppermute | solution.py:80
  96.7 3.4 %collective-permute-start.8 = (bf16[256,1024]{1,0:T(8,128)(2,1)S(1)}, bf16[256,1024]{1,0:T(8,128)(2,1)S(1)}, u32[]{:S(2)}, u32[]{:S(2)}) collective-permute-start(bf16[256,1024]{1,0:T(8,128)(2,1)S(1)} %collective-permute-done.6.rest_3_), channel_id=1, source_target_pairs={{0,128},{128,256},{256,384},{384,512},{512,640},{640,768},{768,896... | collective-permute-start | bytes 1572872 | tf_op jit(solution)/shard_map/ppermute | solution.py:79
  100.1 10.1 %collective-permute-done.9.odd_ref.rest_6_ = bf16[256,1024]{1,0:T(8,128)(2,1)S(1)} collective-permute-done((bf16[256,1024]{1,0:T(8,128)(2,1)S(1)}, bf16[256,1024]{1,0:T(8,128)(2,1)S(1)}, u32[]{:S(2)}, u32[]{:S(2)}) %collective-permute-start.9) | collective-permute-done | bytes 524320 | tf_op jit(solution)/shard_map/ppermute | solution.py:80
  110.2 3.1 %collective-permute-done.8.even_ref.rest_5_ = bf16[256,1024]{1,0:T(8,128)(2,1)S(1)} collective-permute-done((bf16[256,1024]{1,0:T(8,128)(2,1)S(1)}, bf16[256,1024]{1,0:T(8,128)(2,1)S(1)}, u32[]{:S(2)}, u32[]{:S(2)}) %collective-permute-start.8) | collective-permute-done | bytes 524320 | tf_op jit(solution)/shard_map/ppermute | solution.py:79
  113.4 2.1 %collective-permute-start.10 = (bf16[256,1024]{1,0:T(8,128)(2,1)S(1)}, bf16[256,1024]{1,0:T(8,128)(2,1)S(1)}, u32[]{:S(2)}, u32[]{:S(2)}) collective-permute-start(bf16[256,1024]{1,0:T(8,128)(2,1)S(1)} %pick.1), channel_id=1, source_target_pairs={{0,128},{1,897},{2,130},{3,899},{4,132},{5,901},{6,134},{7,903},{8... | collective-permute-start | bytes 1572872 | tf_op jit(solution)/shard_map/ppermute | solution.py:88
  115.5 8.1 %collective-permute-done.10.rest_7_ = bf16[256,1024]{1,0:T(8,128)(2,1)S(1)} collective-permute-done((bf16[256,1024]{1,0:T(8,128)(2,1)S(1)}, bf16[256,1024]{1,0:T(8,128)(2,1)S(1)}, u32[]{:S(2)}, u32[]{:S(2)}) %collective-permute-start.10) | collective-permute-done | bytes 524320 | tf_op jit(solution)/shard_map/ppermute | solution.py:88
  123.6 2.4 %first.1 = (bf16[1024,384]{1,0:T(8,128)(2,1)S(1)}, bf16[2048,1024]{1,0:T(8,128)(2,1)S(1)}) custom-call(bf16[2048,384]{1,0:T(8,128)(2,1)S(1)} %assemble.1.rows_ref, bf16[256,1024]{1,0:T(8,128)(2,1)S(1)} %bitcast.8, bf16[256,1024]{1,0:T(8,128)(2,1)S(1)} %collective-permute-done.4.rest_1_, bf16[256,1024]{1,0:T(8,128)(2,1)S(1)} %collective-permute-done.5.rest_2_, ...), custom_call_target="tpu_custom_call" | custom-call | tf_op jit(solution)/shard_map/first/pallas_call | solution.py:207
  126.0 3.1 %second.1 = bf16[1024,768]{1,0:T(8,128)(2,1)} custom-call(bf16[2048,384]{1,0:T(8,128)(2,1)S(1)} %collective-permute-done.3.rows_ref, bf16[2048,1024]{1,0:T(8,128)(2,1)S(1)} %get-tuple-element.7.hidden_ref, bf16[1024,384]{1,0:T(8,128)(2,1)S(1)} %get-tuple-element.8.done_ref), custom_call_target="tpu_custom_call" | custom-call | tf_op jit(solution)/shard_map/second/pallas_call | solution.py:218
  (10 shorter events, 0.1 us)
Async XLA Ops:
  0.0 52.6 %copy-start = (bf16[1,256,1024]{2,1,0:T(8,128)(2,1)S(1)}, bf16[1,256,1024]{2,1,0:T(8,128)(2,1)}, u32[]{:S(2)}) copy-start(bf16[1,256,1024]{2,1,0:T(8,128)(2,1)} %param.7) | copy-start | bytes 1572868
  45.3 18.0 %all-to-all-start.2 = ((bf16[8,2,32,384]{3,2,1,0:T(8,128)(2,1)}), bf16[8,2,32,384]{3,2,1,0:T(8,128)(2,1)S(1)}, u32[]{:S(2)}, u32[]{:S(2)}) async-start(bf16[8,2,32,384]{3,2,1,0:T(8,128)(2,1)} %all_to_all.16), calls=%async_computation.2 | async-start | bytes 786432 | tf_op jit(solution)/shard_map/all_to_all | solution.py:190
  52.6 20.4 %collective-permute-start.5 = (bf16[256,1024]{1,0:T(8,128)(2,1)S(1)}, bf16[256,1024]{1,0:T(8,128)(2,1)S(1)}, u32[]{:S(2)}, u32[]{:S(2)}) collective-permute-start(bf16[256,1024]{1,0:T(8,128)(2,1)S(1)} %bitcast.6), channel_id=1, source_target_pairs={{0,896},{128,0},{256,128},{384,256},{512,384},{640,512},{768,640},... | collective-permute-start | bytes 1572872 | tf_op jit(solution)/shard_map/ppermute | solution.py:80
  57.2 20.2 %collective-permute-start.4 = (bf16[256,1024]{1,0:T(8,128)(2,1)S(1)}, bf16[256,1024]{1,0:T(8,128)(2,1)S(1)}, u32[]{:S(2)}, u32[]{:S(2)}) collective-permute-start(bf16[256,1024]{1,0:T(8,128)(2,1)S(1)} %bitcast.7), channel_id=1, source_target_pairs={{0,128},{128,256},{256,384},{384,512},{512,640},{640,768},{768,896... | collective-permute-start | bytes 1572872 | tf_op jit(solution)/shard_map/ppermute | solution.py:79
  63.4 15.9 %collective-permute-start.2 = (bf16[8,2,32,384]{3,2,1,0:T(8,128)(2,1)S(1)}, bf16[8,2,32,384]{3,2,1,0:T(8,128)(2,1)S(1)}, u32[]{:S(2)}, u32[]{:S(2)}) collective-permute-start(bf16[8,2,32,384]{3,2,1,0:T(8,128)(2,1)S(1)} %all-to-all-done.2.refs_0_), channel_id=1, source_target_pairs={{0,4},{1,13},{2,6},{3,15},{4,8},{5,1},{6,10},{7,3},{8,12},{9,5},{1... | collective-permute-start | bytes 1179656 | tf_op jit(solution)/shard_map/ppermute | solution.py:193
  67.7 12.5 %collective-permute-start.1 = (bf16[8,2,32,384]{3,2,1,0:T(8,128)(2,1)S(1)}, bf16[8,2,32,384]{3,2,1,0:T(8,128)(2,1)S(1)}, u32[]{:S(2)}, u32[]{:S(2)}) collective-permute-start(bf16[8,2,32,384]{3,2,1,0:T(8,128)(2,1)S(1)} %all-to-all-done.2.refs_0_), channel_id=1, source_target_pairs={{0,14},{1,15},{2,0},{3,1},{4,2},{5,3},{6,4},{7,5},{8,6},{9,7},{10,... | collective-permute-start | bytes 1179656 | tf_op jit(solution)/shard_map/ppermute | solution.py:192
  69.6 16.3 %collective-permute-start = (bf16[8,2,32,384]{3,2,1,0:T(8,128)(2,1)S(1)}, bf16[8,2,32,384]{3,2,1,0:T(8,128)(2,1)S(1)}, u32[]{:S(2)}, u32[]{:S(2)}) collective-permute-start(bf16[8,2,32,384]{3,2,1,0:T(8,128)(2,1)S(1)} %all-to-all-done.2.refs_0_), channel_id=1, source_target_pairs={{0,2},{1,3},{2,4},{3,5},{4,6},{5,7},{6,8},{7,9},{8,10},{9,11},{10,... | collective-permute-start | bytes 1179656 | tf_op jit(solution)/shard_map/ppermute | solution.py:191
  73.0 21.8 %collective-permute-start.7 = (bf16[256,1024]{1,0:T(8,128)(2,1)S(1)}, bf16[256,1024]{1,0:T(8,128)(2,1)S(1)}, u32[]{:S(2)}, u32[]{:S(2)}) collective-permute-start(bf16[256,1024]{1,0:T(8,128)(2,1)S(1)} %collective-permute-done.5.rest_2_), channel_id=1, source_target_pairs={{0,896},{128,0},{256,128},{384,256},{512,384},{640,512},{768,640},... | collective-permute-start | bytes 1572872 | tf_op jit(solution)/shard_map/ppermute | solution.py:80
  77.4 19.4 %collective-permute-start.6 = (bf16[256,1024]{1,0:T(8,128)(2,1)S(1)}, bf16[256,1024]{1,0:T(8,128)(2,1)S(1)}, u32[]{:S(2)}, u32[]{:S(2)}) collective-permute-start(bf16[256,1024]{1,0:T(8,128)(2,1)S(1)} %collective-permute-done.4.rest_1_), channel_id=1, source_target_pairs={{0,128},{128,256},{256,384},{384,512},{512,640},{640,768},{768,896... | collective-permute-start | bytes 1572872 | tf_op jit(solution)/shard_map/ppermute | solution.py:79
  86.1 39.8 %collective-permute-start.3 = (bf16[2048,384]{1,0:T(8,128)(2,1)S(1)}, bf16[2048,384]{1,0:T(8,128)(2,1)S(1)}, u32[]{:S(2)}, u32[]{:S(2)}) collective-permute-start(bf16[2048,384]{1,0:T(8,128)(2,1)S(1)} %assemble.1.rows_ref), channel_id=1, source_target_pairs={{0,1},{1,0},{2,3},{3,2},{4,5},{5,4},{6,7},{7,6},{8,9},{9,8},{10,11... | collective-permute-start | bytes 4718600 | tf_op jit(solution)/shard_map/ppermute | solution.py:204
  94.8 15.4 %collective-permute-start.9 = (bf16[256,1024]{1,0:T(8,128)(2,1)S(1)}, bf16[256,1024]{1,0:T(8,128)(2,1)S(1)}, u32[]{:S(2)}, u32[]{:S(2)}) collective-permute-start(bf16[256,1024]{1,0:T(8,128)(2,1)S(1)} %collective-permute-done.7.rest_4_), channel_id=1, source_target_pairs={{0,896},{128,0},{256,128},{384,256},{512,384},{640,512},{768,640},... | collective-permute-start | bytes 1572872 | tf_op jit(solution)/shard_map/ppermute | solution.py:80
  96.7 16.6 %collective-permute-start.8 = (bf16[256,1024]{1,0:T(8,128)(2,1)S(1)}, bf16[256,1024]{1,0:T(8,128)(2,1)S(1)}, u32[]{:S(2)}, u32[]{:S(2)}) collective-permute-start(bf16[256,1024]{1,0:T(8,128)(2,1)S(1)} %collective-permute-done.6.rest_3_), channel_id=1, source_target_pairs={{0,128},{128,256},{256,384},{384,512},{512,640},{640,768},{768,896... | collective-permute-start | bytes 1572872 | tf_op jit(solution)/shard_map/ppermute | solution.py:79
  113.4 10.2 %collective-permute-start.10 = (bf16[256,1024]{1,0:T(8,128)(2,1)S(1)}, bf16[256,1024]{1,0:T(8,128)(2,1)S(1)}, u32[]{:S(2)}, u32[]{:S(2)}) collective-permute-start(bf16[256,1024]{1,0:T(8,128)(2,1)S(1)} %pick.1), channel_id=1, source_target_pairs={{0,128},{1,897},{2,130},{3,899},{4,132},{5,901},{6,134},{7,903},{8... | collective-permute-start | bytes 1572872 | tf_op jit(solution)/shard_map/ppermute | solution.py:88
